TPU v7x, 8 devices: a whole 2x2x1 slice. The times are simulated.
8 devices in a mesh: dp: 4 (over z, y, x), tp: 2 (over core).
Axes of the slice: x: 2, y: 2, z: 1, core: 2. Of those that a mesh axis runs over, the one named last changes fastest.
Arguments:
- node_lat: bfloat16 [64, 42, 512], P('dp', None, 'tp')
- edge_lat: bfloat16 [64, 300, 512], P('dp', None, 'tp')
- senders: int32 [300], replicated
- receivers: int32 [300], replicated
- grad_node: bfloat16 [64, 42, 512], P('dp', None, 'tp')
- grad_edge: bfloat16 [64, 300, 512], P('dp', None, 'tp')
- edge_w1: bfloat16 [2, 3, 512, 512], P(None, None, 'tp')
- edge_b1: float32 [2, 512], replicated
- edge_w2: bfloat16 [2, 512, 512], P(None, None, 'tp')
- edge_vec: float32 [2, 3, 512], P(None, None, 'tp')
- node_w1: bfloat16 [2, 2, 512, 512], P(None, None, 'tp')
- node_b1: float32 [2, 512], replicated
- node_w2: bfloat16 [2, 512, 512], P(None, None, 'tp')
- node_vec: float32 [2, 3, 512], P(None, None, 'tp')
Outputs:
- output 1: bfloat16 [64, 42, 512], P('dp', None, 'tp')
- output 2: bfloat16 [64, 300, 512], P('dp', None, 'tp')
- output 3: bfloat16 [64, 42, 512], P('dp', None, 'tp')
- output 4: bfloat16 [64, 300, 512], P('dp', None, 'tp')
- output 5: float32 [2, 3, 512, 512], P(None, None, 'tp')
- output 6: float32 [2, 512], replicated
- output 7: float32 [2, 512, 512], P(None, None, 'tp')
- output 8: float32 [2, 3, 512], P(None, None, 'tp')
- output 9: float32 [2, 2, 512, 512], P(None, None, 'tp')
- output 10: float32 [2, 512], replicated
- output 11: float32 [2, 512, 512], P(None, None, 'tp')
- output 12: float32 [2, 3, 512], P(None, None, 'tp')
All inputs are finite; a program needn't handle non-finite values.
Results may differ from a plain program's by a relative error of at most 0.02.
Values sent between devices are 32-bit elements.
A program may use at most 1 GiB of HBM per device.

v0:
```python
import jax
import jax.numpy as jnp
from jax import lax
from jax.sharding import PartitionSpec as P

LN_EPS = 1e-5


def swish_grad(hidden):
    sigmoid_h = jax.nn.sigmoid(hidden)
    return sigmoid_h * (1.0 + hidden * (1.0 - sigmoid_h))


def seg_sum(msg_rows, seg_ids, num_segments):
    def one_sample(sample_rows):
        return jax.ops.segment_sum(sample_rows, seg_ids, num_segments=num_segments)
    return jax.vmap(one_sample)(msg_rows)


def mlp_forward(inputs, w_first, b_first, w_second, norm_vec):
    part_sum = jnp.einsum('bri,ih->brh', inputs[0], w_first[0], preferred_element_type=jnp.float32)
    for block_id in range(1, len(inputs)):
        part_sum = part_sum + jnp.einsum('bri,ih->brh', inputs[block_id], w_first[block_id], preferred_element_type=jnp.float32)
    hidden = lax.psum(part_sum, 'tp') + b_first
    act_bf = jax.nn.silu(hidden).astype(jnp.bfloat16)
    out_f32 = jnp.einsum('brh,ho->bro', act_bf, w_second, preferred_element_type=jnp.float32) + norm_vec[0]
    full_width = w_second.shape[0]
    row_mean = lax.psum(jnp.sum(out_f32, axis=-1, keepdims=True), 'tp') / full_width
    centered = out_f32 - row_mean
    row_var = lax.psum(jnp.sum(centered * centered, axis=-1, keepdims=True), 'tp') / full_width
    inv_std = lax.rsqrt(row_var + LN_EPS)
    normed = centered * inv_std
    message = (normed * norm_vec[1] + norm_vec[2]).astype(jnp.bfloat16)
    return message, (hidden, normed, inv_std)


def mlp_backward(d_message, inputs, w_first, w_second, norm_vec, saved):
    hidden, normed, inv_std = saved
    full_width = w_second.shape[0]
    d_gamma = jnp.sum(d_message * normed, axis=(0, 1))
    d_beta = jnp.sum(d_message, axis=(0, 1))
    d_normed = d_message * norm_vec[1]
    row_stats = lax.psum(jnp.stack([jnp.sum(d_normed, axis=-1), jnp.sum(d_normed * normed, axis=-1)], axis=-1), 'tp') / full_width
    d_out = inv_std * (d_normed - row_stats[..., 0:1] - normed * row_stats[..., 1:2])
    d_out_bf = d_out.astype(jnp.bfloat16)
    act_bf = jax.nn.silu(hidden).astype(jnp.bfloat16)
    d_w_second = jnp.einsum('brh,bro->ho', act_bf, d_out_bf, preferred_element_type=jnp.float32)
    d_act = lax.psum(jnp.einsum('bro,ho->brh', d_out_bf, w_second, preferred_element_type=jnp.float32), 'tp')
    d_hidden = d_act * swish_grad(hidden)
    d_hidden_bf = d_hidden.astype(jnp.bfloat16)
    d_w_first = jnp.stack([jnp.einsum('bri,brh->ih', x_in, d_hidden_bf, preferred_element_type=jnp.float32) for x_in in inputs])
    d_inputs = [jnp.einsum('brh,ih->bri', d_hidden_bf, w_first[block_id], preferred_element_type=jnp.float32) for block_id in range(len(inputs))]
    d_vec = jnp.stack([jnp.sum(d_out, axis=(0, 1)), d_gamma, d_beta])
    return d_inputs, (d_w_first, jnp.sum(d_hidden, axis=(0, 1)), d_w_second, d_vec)


def layer_forward(node_lat, edge_lat, senders, receivers, layer_par):
    send_lat = jnp.take(node_lat, senders, axis=1)
    recv_lat = jnp.take(node_lat, receivers, axis=1)
    edge_inputs = (edge_lat, send_lat, recv_lat)
    edge_msg, edge_saved = mlp_forward(edge_inputs, layer_par[0], layer_par[1], layer_par[2], layer_par[3])
    node_agg = seg_sum(edge_msg.astype(jnp.float32), receivers, node_lat.shape[1]).astype(jnp.bfloat16)
    node_inputs = (node_lat, node_agg)
    node_msg, node_saved = mlp_forward(node_inputs, layer_par[4], layer_par[5], layer_par[6], layer_par[7])
    new_node = (node_lat.astype(jnp.float32) + node_msg.astype(jnp.float32)).astype(jnp.bfloat16)
    new_edge = (edge_lat.astype(jnp.float32) + edge_msg.astype(jnp.float32)).astype(jnp.bfloat16)
    return new_node, new_edge, (edge_inputs, edge_saved, node_inputs, node_saved)


def layer_backward(d_node_out, d_edge_out, senders, receivers, layer_par, layer_saved):
    edge_inputs, edge_saved, node_inputs, node_saved = layer_saved
    d_node = d_node_out.astype(jnp.float32)
    d_edge = d_edge_out.astype(jnp.float32)
    node_din, node_grads = mlp_backward(d_node, node_inputs, layer_par[4], layer_par[6], layer_par[7], node_saved)
    d_edge_msg = d_edge + jnp.take(node_din[1], receivers, axis=1)
    edge_din, edge_grads = mlp_backward(d_edge_msg, edge_inputs, layer_par[0], layer_par[2], layer_par[3], edge_saved)
    num_nodes = d_node.shape[1]
    d_node_in = d_node + node_din[0] + seg_sum(edge_din[1], senders, num_nodes) + seg_sum(edge_din[2], receivers, num_nodes)
    d_edge_in = d_edge + edge_din[0]
    return d_node_in.astype(jnp.bfloat16), d_edge_in.astype(jnp.bfloat16), edge_grads + node_grads


def solution(mesh):
    lat_spec = P('dp', None, 'tp')
    first_spec = P(None, None, 'tp', None)
    col_spec = P(None, None, 'tp')
    param_specs = (first_spec, P(), col_spec, col_spec, first_spec, P(), col_spec, col_spec)
    in_specs = (lat_spec, lat_spec, P(), P(), lat_spec, lat_spec) + param_specs
    out_specs = (lat_spec, lat_spec, lat_spec, lat_spec) + param_specs

    def local_step(node_lat, edge_lat, senders, receivers, grad_node, grad_edge, edge_w1, edge_b1, edge_w2, edge_vec, node_w1, node_b1, node_w2, node_vec):
        params = (edge_w1, edge_b1, edge_w2, edge_vec, node_w1, node_b1, node_w2, node_vec)
        num_layers = edge_w1.shape[0]
        saved_all = []
        for layer_id in range(num_layers):
            layer_par = tuple(par_arr[layer_id] for par_arr in params)
            node_lat, edge_lat, layer_saved = layer_forward(node_lat, edge_lat, senders, receivers, layer_par)
            saved_all.append(layer_saved)
        d_node = grad_node
        d_edge = grad_edge
        grads_rev = []
        for layer_id in reversed(range(num_layers)):
            layer_par = tuple(par_arr[layer_id] for par_arr in params)
            d_node, d_edge, layer_grads = layer_backward(d_node, d_edge, senders, receivers, layer_par, saved_all[layer_id])
            grads_rev.append(layer_grads)
        grads_fwd = grads_rev[::-1]
        param_grads = tuple(
            lax.psum(jnp.stack([layer_grads[par_id] for layer_grads in grads_fwd]), 'dp')
            for par_id in range(len(params)))
        return (node_lat, edge_lat, d_node, d_edge) + param_grads

    return jax.shard_map(local_step, mesh=mesh, in_specs=in_specs, out_specs=out_specs, check_vma=False)
```

profile of v0, /device:TPU:0, one launch (start us, length us, event | category | flops | bytes accessed | tf_op | source)
XLA Modules:
  0.0 754.4 jit_solution(14741096074903320825)
XLA Ops:
  24.8 8.5 %add_add_fusion.1 = f32[16,300,512]{2,1,0:T(8,128)} fusion(f32[16,300,512]{2,1,0:T(8,128)S(1)} %fusion.20, f32[16,300,512]{2,1,0:T(8,128)S(1)} %fusion.16, bf16[16,300,256]{2,0,1:T(8,128)(2,1)} %select_bitcast_fusion.2, bf16[2,3,256,512]{3,2,1,0:T(8,128)(2,1)} %param.24), kind=kOutput, calls=%fused_computation.19 | convolution fusion | flops 1263206400 | bytes 32210944 | tf_op jit(solution)/shard_map/bri,ih->brh/dot_general | solution.py:23
  37.1 32.0 %all-reduce.12.cloned.1.call-done = f32[16,300,512]{2,1,0:T(8,128)} async-done(((f32[16,300,512]{2,1,0:T(8,128)}), f32[16,300,512]{2,1,0:T(8,128)}) %all-reduce.12.cloned.1.call-update) | async-done | bytes 9830416 | tf_op jit(solution)/shard_map/psum | solution.py:24
  69.1 6.5 multiply_convert_fusion.1
  75.6 3.7 add_reduce_fusion.1
  89.7 4.5 fusion
  94.3 5.1 copy.70
  99.5 27.3 %scatter_fusion = f32[16,42,256]{2,0,1:T(8,128)S(1)} fusion(f32[16,42,256]{2,0,1:T(8,128)S(1)} %broadcast.51.clone, s32[300]{0:T(512)S(1)} %copy-done.73, f32[300,16,256]{2,1,0:T(8,128)} %copy.70), kind=kCustom, calls=%fused_computation.6 | custom fusion | flops 1228800 | bytes 14746800 | tf_op jit(solution)/shard_map/vmap()/scatter-add | solution.py:16
  132.4 6.2 fusion.86
  138.5 7.7 %all-reduce.14.cloned.1.call-done = f32[16,42,512]{2,1,0:T(8,128)} async-done(((f32[16,42,512]{2,1,0:T(8,128)}), f32[16,42,512]{2,1,0:T(8,128)}) %all-reduce.14.cloned.1.call-update) | async-done | bytes 1376272 | tf_op jit(solution)/shard_map/psum | solution.py:24
  163.2 4.3 select_bitcast_fusion
  170.3 8.5 %add_add_fusion = f32[16,300,512]{2,1,0:T(8,128)} fusion(f32[16,300,512]{2,1,0:T(8,128)S(1)} %bitcast.339, f32[16,300,512]{2,1,0:T(8,128)S(1)} %fusion.13, bf16[16,300,256]{2,0,1:T(8,128)(2,1)} %select_bitcast_fusion, bf16[2,3,256,512]{3,2,1,0:T(8,128)(2,1)} %param.24), kind=kOutput, calls=%fused_computation.16 | convolution fusion | flops 1263206400 | bytes 32210944 | tf_op jit(solution)/shard_map/bri,ih->brh/dot_general | solution.py:23
  181.6 31.4 %all-reduce.16.cloned.1.call-done = f32[16,300,512]{2,1,0:T(8,128)} async-done(((f32[16,300,512]{2,1,0:T(8,128)}), f32[16,300,512]{2,1,0:T(8,128)}) %all-reduce.16.cloned.1.call-update) | async-done | bytes 9830416 | tf_op jit(solution)/shard_map/psum | solution.py:24
  213.0 6.5 multiply_convert_fusion
  219.5 3.8 add_reduce_fusion
  233.9 5.2 fusion.1
  239.1 5.1 copy.77
  244.4 27.3 %scatter_fusion.1 = f32[16,42,256]{2,0,1:T(8,128)S(1)} fusion(f32[16,42,256]{2,0,1:T(8,128)S(1)} %broadcast.51.clone.1, s32[300]{0:T(512)S(1)} %copy-done.74, f32[300,16,256]{2,1,0:T(8,128)} %copy.77), kind=kCustom, calls=%fused_computation.7 | custom fusion | flops 1228800 | bytes 14746800 | tf_op jit(solution)/shard_map/vmap()/scatter-add | solution.py:16
  275.0 15.5 %all-reduce.18.cloned.1.call-done = f32[16,42,512]{2,1,0:T(8,128)} async-done(((f32[16,42,512]{2,1,0:T(8,128)}), f32[16,42,512]{2,1,0:T(8,128)}) %all-reduce.18.cloned.1.call-update) | async-done | bytes 1376272 | tf_op jit(solution)/shard_map/psum | solution.py:24
  306.3 15.5 %all-reduce.20.cloned.1.call-done = f32[16,42,512]{2,1,0:T(8,128)} async-done(((f32[16,42,512]{2,1,0:T(8,128)}), f32[16,42,512]{2,1,0:T(8,128)}) %all-reduce.20.cloned.1.call-update) | async-done | bytes 1376272 | tf_op jit(solution)/shard_map/psum | solution.py:48
  329.0 8.8 %multiply_reduce_fusion = (f32[256]{0:T(256)}, f32[16,300]{1,0:T(8,128)S(1)}, f32[16,300]{1,0:T(8,128)S(1)}, f32[256]{0:T(256)}) fusion(f32[16,300]{1,0:T(8,128)S(1)} %copy-done.60, f32[16,300]{1,0:T(8,128)S(1)} %copy-done.53, f32[16,300,256]{2,1,0:T(8,128)} %get-tuple-element.112, f32[256]{0:T(256)S(1)} %bitcast.349, f32[300,16,256]{2,1,0:T(8,128)} %gather_fusion.4, ...), kind=kLoop, calls=%fused_computation.34 | loop fusion | flops 15964288 | bytes 12369196 | tf_op jit(solution)/shard_map/reduce_sum | solution.py:40
  341.4 10.4 %fusion.150 = (f32[256]{0:T(256)}, bf16[16,300,256]{2,1,0:T(8,128)(2,1)S(1)}) fusion(f32[16,300]{1,0:T(8,128)S(1)} %get-tuple-element.86, f32[16,300]{1,0:T(8,128)S(1)} %copy-done.53, f32[16,300,256]{2,1,0:T(8,128)} %get-tuple-element.112, f32[256]{0:T(256)S(1)} %bitcast.350, f32[16,300]{1,0:T(8,128)S(1)} %get-tuple-element.85, f32[256]{0:T(256)S(1)} %bitcast.383, ...), kind=kLoop, calls=%fused_computation.269 | loop fusion | flops 15974144 | bytes 14825772 | tf_op jit(solution)/shard_map/reduce_sum | solution.py:53
  353.3 5.3 fusion.28
  359.4 33.3 %all-reduce.22.cloned.1.call-done = f32[16,300,512]{2,1,0:T(8,128)} async-done(((f32[16,300,512]{2,1,0:T(8,128)}), f32[16,300,512]{2,1,0:T(8,128)}) %all-reduce.22.cloned.1.call-update) | async-done | bytes 9830416 | tf_op jit(solution)/shard_map/psum | solution.py:48
  392.7 9.6 %fusion.152 = (f32[512]{0:T(512)}, bf16[16,300,512]{2,1,0:T(8,128)(2,1)S(1)}) fusion(f32[16,300,512]{2,1,0:T(8,128)} %all-reduce.22.cloned.1.call-done, f32[16,300,512]{2,1,0:T(8,128)} %all-reduce.16.cloned.1.call-done, f32[512]{0:T(512)S(1)} %bitcast.373), kind=kLoop, calls=%fused_computation.271 | loop fusion | flops 27033088 | bytes 24580096 | tf_op jit(solution)/shard_map/reduce_sum | solution.py:54
  407.4 5.0 copy.85
  412.4 5.1 copy.84
  417.6 27.3 %scatter_fusion.3 = f32[16,42,256]{2,0,1:T(8,128)S(1)} fusion(f32[16,42,256]{2,0,1:T(8,128)S(1)} %broadcast.51.clone.2, s32[300]{0:T(512)S(1)} %copy-done.74, f32[300,16,256]{2,1,0:T(8,128)} %copy.85), kind=kCustom, calls=%fused_computation.9 | custom fusion | flops 1228800 | bytes 14746800 | tf_op jit(solution)/shard_map/vmap()/scatter-add | solution.py:16
  444.9 27.7 %scatter_fusion.2 = f32[16,42,256]{2,0,1:T(8,128)S(1)} fusion(f32[16,42,256]{2,0,1:T(8,128)S(1)} %copy.83, s32[300]{0:T(512)} %param.20, f32[300,16,256]{2,1,0:T(8,128)} %copy.84), kind=kCustom, calls=%fused_computation.8 | custom fusion | flops 1228800 | bytes 14746800 | tf_op jit(solution)/shard_map/vmap()/scatter-add | solution.py:16
  484.0 15.5 %all-reduce.24.cloned.1.call-done = f32[16,42,512]{2,1,0:T(8,128)} async-done(((f32[16,42,512]{2,1,0:T(8,128)}), f32[16,42,512]{2,1,0:T(8,128)}) %all-reduce.24.cloned.1.call-update) | async-done | bytes 1376272 | tf_op jit(solution)/shard_map/psum | solution.py:48
  507.8 12.3 %multiply_reduce_fusion.1 = (f32[256]{0:T(256)S(1)}, f32[16,300]{1,0:T(8,128)S(1)}, f32[16,300]{1,0:T(8,128)S(1)}, f32[256]{0:T(256)}, bf16[16,300,256]{2,1,0:T(8,128)(2,1)}) fusion(f32[16,300]{1,0:T(8,128)S(1)} %copy-done.62, f32[16,300]{1,0:T(8,128)S(1)} %copy-done.58, f32[16,300,256]{2,1,0:T(8,128)} %get-tuple-element.108, f32[256]{0:T(256)S(1)} %bitcast.362, ...), kind=kOutput, calls=%fused_computation.35 | convolution fusion | flops 1277941760 | bytes 20135212 | tf_op jit(solution)/shard_map/brh,ih->bri/dot_general | solution.py:52
  523.7 6.8 fusion.149
  532.0 5.3 fusion.24
  543.0 4.2 fusion.30
  552.2 4.4 fusion.42
  556.6 4.6 fusion.45
  566.6 4.9 all-reduce.26.cloned.1.call-done
  571.5 8.6 %fusion.151 = (f32[512]{0:T(512)S(1)}, bf16[16,300,512]{2,1,0:T(8,128)(2,1)S(1)}) fusion(f32[16,300,512]{2,1,0:T(8,128)} %all-reduce.26.cloned.1.call-done, f32[16,300,512]{2,1,0:T(8,128)} %all-reduce.12.cloned.1.call-done, f32[512]{0:T(512)S(1)} %bitcast.371), kind=kLoop, calls=%fused_computation.270 | loop fusion | flops 27033088 | bytes 24580096 | tf_op jit(solution)/shard_map/reduce_sum | solution.py:54
  580.2 3.8 fusion.36
  584.0 3.8 fusion.39
  592.7 4.1 copy.110
  605.2 18.1 %all-reduce = (f32[2,512]{1,0:T(2,128)}, f32[2,3,256]{2,1,0:T(4,128)S(1)}, f32[2,512]{1,0:T(2,128)}, f32[2,3,256]{2,1,0:T(4,128)S(1)}) all-reduce(f32[2,512]{1,0:T(2,128)S(1)} %get-tuple-element.124, f32[2,3,256]{2,1,0:T(4,128)S(1)} %pad_maximum_fusion.8, ...), channel_id=1, replica_groups=mesh['dp'=4,'tp'=2] {'dp'}, use_global_device_ids=true, to_apply=%region_45.48 | all-reduce | flops 5120 | bytes 40960 | tf_op jit(solution)/shard_map/psum | solution.py:108
  624.5 4.1 convolution_bitcast_fusion
  628.5 5.1 copy.92
  636.1 5.0 copy.91
  641.2 27.3 %scatter_fusion.5 = f32[16,42,256]{2,0,1:T(8,128)S(1)} fusion(f32[16,42,256]{2,0,1:T(8,128)S(1)} %broadcast.51, s32[300]{0:T(512)S(1)} %copy-done.75, f32[300,16,256]{2,1,0:T(8,128)} %copy.92), kind=kCustom, calls=%fused_computation.11 | custom fusion | flops 1228800 | bytes 14746800 | tf_op jit(solution)/shard_map/vmap()/scatter-add | solution.py:16
  668.6 27.3 %scatter_fusion.4 = f32[16,42,256]{2,0,1:T(8,128)S(1)} fusion(f32[16,42,256]{2,0,1:T(8,128)S(1)} %copy.90, s32[300]{0:T(512)S(1)} %copy-done.80, f32[300,16,256]{2,1,0:T(8,128)} %copy.91), kind=kCustom, calls=%fused_computation.10 | custom fusion | flops 1228800 | bytes 14746800 | tf_op jit(solution)/shard_map/vmap()/scatter-add | solution.py:16
  696.7 42.1 %all-reduce.28.cloned.1.call-done = (f32[2,3,256,512]{2,3,1,0:T(8,128)}, f32[2,512,256]{2,1,0:T(8,128)}, f32[2,2,256,512]{2,3,1,0:T(8,128)}, f32[2,512,256]{2,1,0:T(8,128)}) async-done(((f32[2,3,256,512]{2,3,1,0:T(8,128)}, f32[2,512,256]{2,1,0:T(8,128)}, f32[2,2,256,512]{2,3,1,0:T(8,128)}, f32[2,512,256]{2,1,0:T(8,128)}), (f32[2,3,256,512]{2,3,1,0:T(8,128)}, f32[2,512,256]{2,1,0:T(8,128)}, ...) | async-done | bytes 7340048 | tf_op jit(solution)/shard_map/psum | solution.py:108
  738.8 3.7 copy.112
  (405 shorter events, 170.1 us)
Async XLA Ops:
  7.2 61.9 %all-reduce.12.cloned.1.call-start = ((), (), s32[]{:S(2)}) async-start(), calls=%async_computation | async-start | bytes 19922944 | tf_op jit(solution)/shard_map/psum | solution.py:24
  9.3 153.9 %copy-start.83 = (pred[300]{0:T(512)(128)(4,1)}, pred[300]{0:T(512)(128)(4,1)S(1)}, u32[]{:S(2)}) copy-start(pred[300]{0:T(512)(128)(4,1)S(1)} %compare_and_fusion) | copy-start | bytes 904
  10.1 148.6 %copy-start.78 = (s32[1024]{0:T(1024)}, s32[1024]{0:T(1024)S(1)}, u32[]{:S(2)}) copy-start(s32[1024]{0:T(1024)S(1)} %pad_clamp_fusion) | copy-start | bytes 12292
  33.4 112.9 %all-reduce.14.cloned.1.call-start = ((), (), s32[]{:S(2)}) async-start(), calls=%async_computation.1 | async-start | bytes 3145728 | tf_op jit(solution)/shard_map/psum | solution.py:24
  34.0 41.5 %copy-start.89 = (f32[1,512]{1,0:T(1,128)}, f32[1,512]{1,0:T(1,128)S(1)}, u32[]{:S(2)}) copy-start(f32[1,512]{1,0:T(1,128)S(1)} %get-tuple-element.106) | copy-start | bytes 6148
  34.0 178.9 %copy-start.91 = (f32[1,512]{1,0:T(1,128)}, f32[1,512]{1,0:T(1,128)S(1)}, u32[]{:S(2)}) copy-start(f32[1,512]{1,0:T(1,128)S(1)} %get-tuple-element.105) | copy-start | bytes 6148
  34.6 55.1 %copy-start.81 = (f32[1,1,256]{2,0,1:T(1,128)}, f32[1,1,256]{2,0,1:T(1,128)S(1)}, u32[]{:S(2)}) copy-start(f32[1,1,256]{2,0,1:T(1,128)S(1)} %get-tuple-element.100) | copy-start | bytes 3076
  34.6 55.1 %copy-start.99 = (f32[1,1,256]{2,0,1:T(1,128)}, f32[1,1,256]{2,0,1:T(1,128)S(1)}, u32[]{:S(2)}) copy-start(f32[1,1,256]{2,0,1:T(1,128)S(1)} %get-tuple-element.99) | copy-start | bytes 3076
  34.6 199.3 %copy-start.76 = (f32[1,1,256]{2,0,1:T(1,128)}, f32[1,1,256]{2,0,1:T(1,128)S(1)}, u32[]{:S(2)}) copy-start(f32[1,1,256]{2,0,1:T(1,128)S(1)} %get-tuple-element.97) | copy-start | bytes 3076
  82.7 11.5 %copy-start.57 = (f32[16,300]{1,0:T(8,128)}, f32[16,300]{1,0:T(8,128)S(1)}, u32[]{:S(2)}) copy-start(f32[16,300]{1,0:T(8,128)S(1)} %multiply_bitcast_fusion.1) | copy-start | bytes 57604
  94.3 38.1 %copy-start.9 = (bf16[16,300,256]{2,1,0:T(8,128)(2,1)}, bf16[16,300,256]{2,1,0:T(8,128)(2,1)S(1)}, u32[]{:S(2)}) copy-start(bf16[16,300,256]{2,1,0:T(8,128)(2,1)S(1)} %get-tuple-element.79) | copy-start | bytes 7372804
  130.7 82.3 %all-reduce.16.cloned.1.call-start = ((), (), s32[]{:S(2)}) async-start(), calls=%async_computation.2 | async-start | bytes 19922944 | tf_op jit(solution)/shard_map/psum | solution.py:24
  131.8 14.5 %copy-start.86 = (f32[1,512]{1,0:T(1,128)}, f32[1,512]{1,0:T(1,128)S(1)}, u32[]{:S(2)}) copy-start(f32[1,512]{1,0:T(1,128)S(1)} %get-tuple-element.104) | copy-start | bytes 6148
  138.5 17.2 %copy-start.95 = (f32[1,1,256]{2,0,1:T(1,128)S(1)}, f32[1,1,256]{2,0,1:T(1,128)}, u32[]{:S(2)}) copy-start(f32[1,1,256]{2,0,1:T(1,128)} %get-tuple-element.94) | copy-start | bytes 3076
  138.5 17.2 %copy-start.116 = (f32[1,1,256]{2,0,1:T(1,128)S(1)}, f32[1,1,256]{2,0,1:T(1,128)}, u32[]{:S(2)}) copy-start(f32[1,1,256]{2,0,1:T(1,128)} %get-tuple-element.93) | copy-start | bytes 3076
  156.3 22.8 %copy-start.28 = (bf16[16,42,256]{2,1,0:T(8,128)(2,1)}, bf16[16,42,256]{2,1,0:T(8,128)(2,1)S(1)}, u32[]{:S(2)}) copy-start(bf16[16,42,256]{2,1,0:T(8,128)(2,1)S(1)} %add_convert_fusion.4) | copy-start | bytes 1032196
  178.9 111.5 %all-reduce.18.cloned.1.call-start = ((), (), s32[]{:S(2)}) async-start(), calls=%async_computation.3 | async-start | bytes 3145728 | tf_op jit(solution)/shard_map/psum | solution.py:24
  223.3 10.6 %copy-start.10 = (bf16[16,300,256]{2,1,0:T(8,128)(2,1)S(1)}, bf16[16,300,256]{2,1,0:T(8,128)(2,1)}, u32[]{:S(2)}) copy-start(bf16[16,300,256]{2,1,0:T(8,128)(2,1)} %copy-done.9) | copy-start | bytes 7372804
  223.3 10.6 %copy-start.96 = (f32[1,1,256]{2,0,1:T(1,128)S(1)}, f32[1,1,256]{2,0,1:T(1,128)}, u32[]{:S(2)}) copy-start(f32[1,1,256]{2,0,1:T(1,128)} %get-tuple-element.102) | copy-start | bytes 3076
  223.3 10.6 %copy-start.114 = (f32[1,1,256]{2,0,1:T(1,128)S(1)}, f32[1,1,256]{2,0,1:T(1,128)}, u32[]{:S(2)}) copy-start(f32[1,1,256]{2,0,1:T(1,128)} %get-tuple-element.101) | copy-start | bytes 3076
  226.9 12.2 %copy-start.52 = (f32[16,300]{1,0:T(8,128)}, f32[16,300]{1,0:T(8,128)S(1)}, u32[]{:S(2)}) copy-start(f32[16,300]{1,0:T(8,128)S(1)} %multiply_bitcast_fusion) | copy-start | bytes 57604
  244.4 27.4 %copy-start.35 = (bf16[2,2,256,512]{3,2,1,0:T(8,128)(2,1)S(1)}, bf16[2,2,256,512]{3,2,1,0:T(8,128)(2,1)}, u32[]{:S(2)}) copy-start(bf16[2,2,256,512]{3,2,1,0:T(8,128)(2,1)} %param.28) | copy-start | bytes 3145732
  271.7 18.7 %copy-start.88 = (f32[1,512]{1,0:T(1,128)S(1)}, f32[1,512]{1,0:T(1,128)}, u32[]{:S(2)}) copy-start(f32[1,512]{1,0:T(1,128)} %get-tuple-element.103) | copy-start | bytes 6148
  271.7 20.6 %copy-start.115 = (f32[1,1,256]{2,0,1:T(1,128)S(1)}, f32[1,1,256]{2,0,1:T(1,128)}, u32[]{:S(2)}) copy-start(f32[1,1,256]{2,0,1:T(1,128)} %get-tuple-element.92) | copy-start | bytes 3076
  271.8 18.7 %copy-start.48 = (bf16[16,42,256]{2,0,1:T(8,128)(2,1)}, bf16[16,42,256]{2,0,1:T(8,128)(2,1)S(1)}, u32[]{:S(2)}) copy-start(bf16[16,42,256]{2,0,1:T(8,128)(2,1)S(1)} %convert_element_type.135) | copy-start | bytes 1032196
  271.8 27.7 %copy-start.33 = (bf16[16,42,256]{2,0,1:T(8,128)(2,1)S(1)}, bf16[16,42,256]{2,0,1:T(8,128)(2,1)}, u32[]{:S(2)}) copy-start(bf16[16,42,256]{2,0,1:T(8,128)(2,1)} %param.22) | copy-start | bytes 1032196
  271.8 27.7 %copy-start.93 = (f32[1,1,256]{2,0,1:T(1,128)S(1)}, f32[1,1,256]{2,0,1:T(1,128)}, u32[]{:S(2)}) copy-start(f32[1,1,256]{2,0,1:T(1,128)} %get-tuple-element.91) | copy-start | bytes 3076
  274.9 46.9 %all-reduce.20.cloned.1.call-start = ((), (), s32[]{:S(2)}) async-start(), calls=%async_computation.4 | async-start | bytes 3145728 | tf_op jit(solution)/shard_map/psum | solution.py:48
  292.3 14.0 %copy-start.39 = (bf16[16,42,512]{2,1,0:T(8,128)(2,1)}, bf16[16,42,512]{2,1,0:T(8,128)(2,1)S(1)}, u32[]{:S(2)}) copy-start(bf16[16,42,512]{2,1,0:T(8,128)(2,1)S(1)} %multiply_convert_fusion.2) | copy-start | bytes 2064388
  293.9 31.0 %copy-start.14 = (f32[16,42,256]{2,1,0:T(8,128)}, f32[16,42,256]{2,1,0:T(8,128)S(1)}, u32[]{:S(2)}) copy-start(f32[16,42,256]{2,1,0:T(8,128)S(1)} %get-tuple-element.114) | copy-start | bytes 2064388
  296.4 28.5 %copy-start.63 = (f32[16,42]{1,0:T(8,128)}, f32[16,42]{1,0:T(8,128)S(1)}, u32[]{:S(2)}) copy-start(f32[16,42]{1,0:T(8,128)S(1)} %multiply_bitcast_fusion.2) | copy-start | bytes 8068
  299.5 25.4 %copy-start.66 = (f32[16,42]{1,0:T(8,128)}, f32[16,42]{1,0:T(8,128)S(1)}, u32[]{:S(2)}) copy-start(f32[16,42]{1,0:T(8,128)S(1)} %rsqrt_bitcast_fusion.2) | copy-start | bytes 8068
  303.5 22.0 %copy-start.69 = (f32[16,42]{1,0:T(8,128)}, f32[16,42]{1,0:T(8,128)S(1)}, u32[]{:S(2)}) copy-start(f32[16,42]{1,0:T(8,128)S(1)} %get-tuple-element.89) | copy-start | bytes 8068
  303.5 22.0 %copy-start.71 = (f32[16,42]{1,0:T(8,128)}, f32[16,42]{1,0:T(8,128)S(1)}, u32[]{:S(2)}) copy-start(f32[16,42]{1,0:T(8,128)S(1)} %get-tuple-element.90) | copy-start | bytes 8068
  303.5 22.0 %copy-start.79 = (s32[1024]{0:T(1024)S(1)}, s32[1024]{0:T(1024)}, u32[]{:S(2)}) copy-start(s32[1024]{0:T(1024)} %copy-done.78) | copy-start | bytes 12292
  306.2 86.5 %all-reduce.22.cloned.1.call-start = ((), (), s32[]{:S(2)}) async-start(), calls=%async_computation.5 | async-start | bytes 19922944 | tf_op jit(solution)/shard_map/psum | solution.py:48
  324.9 33.7 %copy-start.16 = (bf16[16,42,512]{2,1,0:T(8,128)(2,1)}, bf16[16,42,512]{2,1,0:T(8,128)(2,1)S(1)}, u32[]{:S(2)}) copy-start(bf16[16,42,512]{2,1,0:T(8,128)(2,1)S(1)} %get-tuple-element.67) | copy-start | bytes 2064388
  341.4 11.8 %copy-start.43 = (bf16[2,512,256]{2,1,0:T(8,128)(2,1)S(1)}, bf16[2,512,256]{2,1,0:T(8,128)(2,1)}, u32[]{:S(2)}) copy-start(bf16[2,512,256]{2,1,0:T(8,128)(2,1)} %param.26) | copy-start | bytes 1572868
  358.5 34.2 %copy-start.92 = (f32[1,512]{1,0:T(1,128)S(1)}, f32[1,512]{1,0:T(1,128)}, u32[]{:S(2)}) copy-start(f32[1,512]{1,0:T(1,128)} %copy-done.91) | copy-start | bytes 6148
  358.6 141.0 %all-reduce.24.cloned.1.call-start = ((), (), s32[]{:S(2)}) async-start(), calls=%async_computation.6 | async-start | bytes 3145728 | tf_op jit(solution)/shard_map/psum | solution.py:48
  444.9 27.8 %copy-start.13 = (f32[16,42,256]{2,1,0:T(8,128)S(1)}, f32[16,42,256]{2,1,0:T(8,128)}, u32[]{:S(2)}) copy-start(f32[16,42,256]{2,1,0:T(8,128)} %copy-done.12) | copy-start | bytes 2064388
  475.2 24.4 %copy-start.87 = (f32[1,512]{1,0:T(1,128)S(1)}, f32[1,512]{1,0:T(1,128)}, u32[]{:S(2)}) copy-start(f32[1,512]{1,0:T(1,128)} %copy-done.86) | copy-start | bytes 6148
  484.0 87.5 %all-reduce.26.cloned.1.call-start = ((), (), s32[]{:S(2)}) async-start(), calls=%async_computation.7 | async-start | bytes 19922944 | tf_op jit(solution)/shard_map/psum | solution.py:48
  537.4 201.4 %all-reduce.28.cloned.1.call-start = ((), (), s32[]{:S(2)}) async-start(), calls=%async_computation.8 | async-start | bytes 14680064 | tf_op jit(solution)/shard_map/psum | solution.py:108
  566.6 13.6 %copy-start.21 = (bf16[16,300,256]{2,0,1:T(8,128)(2,1)S(1)}, bf16[16,300,256]{2,0,1:T(8,128)(2,1)}, u32[]{:S(2)}) copy-start(bf16[16,300,256]{2,0,1:T(8,128)(2,1)} %copy-done.20) | copy-start | bytes 7372804
  602.9 30.8 %slice-start.4 = ((s8[4980736]{0:T(1024)(128)(4,1)}), s8[786432]{0:T(1024)(128)(4,1)S(1)}, s32[]{:S(2)}) async-start(s8[4980736]{0:T(1024)(128)(4,1)} %bitcast.334), calls=%async_computation.13 | async-start | bytes 1572864
  624.5 9.2 %slice-start.5 = ((s8[4980736]{0:T(1024)(128)(4,1)}), s8[4194304]{0:T(1024)(128)(4,1)S(1)}, s32[]{:S(2)}) async-start(s8[4980736]{0:T(1024)(128)(4,1)} %bitcast.334), calls=%async_computation.14 | async-start | bytes 8388608
  641.2 27.3 %copy-start.80 = (s32[300]{0:T(512)S(1)}, s32[300]{0:T(512)}, u32[]{:S(2)}) copy-start(s32[300]{0:T(512)} %param.20) | copy-start | bytes 3604
  (92 other events, 387.7 us)
Sparse Core Ops, SparseCore 0:
  33.5 35.5 all-reduce.11
  130.8 15.3 all-reduce.13
  179.0 33.9 all-reduce.15
  275.0 15.3 all-reduce.17
  306.4 15.3 all-reduce.19
  358.7 33.9 all-reduce.21
  484.1 15.4 all-reduce.23
  537.5 33.9 all-reduce.25
  592.7 146.0 all-reduce.27
where the time goes:
time: 766 us; the launch traced here: 754 us
  other arithmetic  274 us (36%)
  waiting for transfers between devices  198 us (26%)
  matrix products  132 us (17%)
  local copies, waits for them, and re-layouts  76.9 us (10%)
  blocking collectives  56.4 us (7%)
  between operations  16.1 us (2%)
    scatter-add x6, other arithmetic, one_sample(): return jax.ops.segment_sum(sample_rows, seg_ids, num_segments=num_segments)  164 us
    psum x4, waiting for transfers between devices, mlp_forward(): hidden = lax.psum(part_sum, 'tp') + b_first  86.5 us
    psum x4, waiting for transfers between devices, mlp_backward(): lax.psum(jnp.einsum('bro,ho->brh', d_out_bf, w_second, preferred_element_...  69.2 us
    psum x1, waiting for transfers between devices, local_step(): lax.psum(jnp.stack([layer_grads[par_id] for layer_grads in grads_fwd]), '...  42.1 us
    dot_general x10, matrix products, mlp_backward(): jnp.einsum('brh,ih->bri', d_hidden_bf, w_first[block_id], preferred_eleme...  29.1 us
    dot_general x6, matrix products, mlp_forward(): jnp.einsum('bri,ih->brh', inputs[block_id], w_first[block_id], preferred_...  29 us
    unnamed x271, local copies, waits for them, and re-layouts  25.4 us
    dot_general x10, matrix products, mlp_backward(): jnp.einsum('bri,brh->ih', x_in, d_hidden_bf, preferred_element_type=jnp.f...  25.1 us
  transfers between devices with their start and end apart: 9, of which 9 were waited for; matrix products, arithmetic and copies ran while one was open for 17% of the time, Pallas kernels for 0%

commit v1 on v0

v1 whole, which is shorter than its diff:
```python
import functools

import jax
import jax.numpy as jnp
from jax import lax
from jax.experimental import pallas as pl
from jax.experimental.pallas import tpu as pltpu
from jax.sharding import PartitionSpec as P

BF = jnp.bfloat16
F32 = jnp.float32
MESH = pl.DeviceIdType.MESH
LN_EPS = 1e-5
NS = 8
NN = 42
NP = 48
NE = 300
D = 512
H = 256
ROWS = NS * NP


def dot(lhs, rhs, lc=1, rc=0):
    return lax.dot_general(lhs, rhs, (((lc,), (rc,)), ((), ())), preferred_element_type=F32)


def split3(x):
    hi = x.astype(BF)
    rest = x - hi.astype(F32)
    mid = rest.astype(BF)
    low = (rest - mid.astype(F32)).astype(BF)
    return hi, mid, low


def cat(lhs, rhs):
    return jnp.concatenate([lhs, rhs], axis=1)


def mean_cols(x):
    return jnp.sum(x, axis=1, keepdims=True) * (1.0 / D)


def sum_rows(x):
    return jnp.sum(x, axis=0, keepdims=True)


def norm_parts(centered):
    inv_std = lax.rsqrt(mean_cols(centered * centered) + LN_EPS)
    return centered * inv_std, inv_std


J_NW2, J_NW1, J_EW2, J_EW1 = 0, 1, 3, 4


def body(nl, el, gn, ge, w1e, w2e, w1n, w2n, b1e, b1n, vece, vecn, snd, rcv,
         o_n, o_e, o_dn, o_de, o_g, o_sm, spill,
         W1E, W2E, W1N, W2N, VE, VN, S3, R3, TT,
         E0, E1, E2, DE, HS, CS, R2, G, PS, PR,
         NST, NF, VF, SF, HN, CN, DN, DV, GS, GR, SM,
         lsem, ssem, rsem, csem, spsem):
    dp = lax.axis_index('dp')
    tp = lax.axis_index('tp')
    ot = 1 - tp
    partner = (dp, ot)

    def rdma(src, dst, idx):
        return pltpu.make_async_remote_copy(
            src_ref=src, dst_ref=dst, send_sem=ssem.at[idx], recv_sem=rsem.at[idx],
            device_id=partner, device_id_type=MESH)

    mine = pl.ds(tp * NS, NS)
    theirs = pl.ds(ot * NS, NS)
    loads = [
        (nl.at[mine], NST.at[0]), (nl.at[theirs], NST.at[1]),
        (w1e, W1E.at[:, :, tp]), (el.at[theirs], E1.at[:, 0]), (w2e, W2E.at[:, tp]),
        (el.at[mine], E0.at[:, tp]), (w1n, W1N.at[:, :, tp]), (w2n, W2N.at[:, tp]),
        (ge.at[theirs], E1.at[:, 1]), (ge.at[mine], DE.at[:, tp]),
        (gn.at[mine], NST.at[2]), (gn.at[theirs], NST.at[3]),
    ]
    loads = [pltpu.make_async_copy(src, dst, lsem.at[i]) for i, (src, dst) in enumerate(loads)]
    for cp in loads:
        cp.start()

    barrier = pltpu.get_barrier_semaphore()
    pl.semaphore_signal(barrier, inc=1, device_id=partner, device_id_type=MESH)

    for base, ids in ((0, snd), (NP, rcv)):
        rows = lax.broadcasted_iota(jnp.int32, (NP, NE), 0)
        TT[base:base + NP] = jnp.where(rows == ids[...], 1.0, 0.0).astype(BF)
    row_i = lax.broadcasted_iota(jnp.int32, (NP, 3 * NP), 0)
    col_i = lax.broadcasted_iota(jnp.int32, (NP, 3 * NP), 1)
    eye3 = jnp.where((col_i == row_i) | (col_i == row_i + NP) | (col_i == row_i + 2 * NP), 1.0, 0.0).astype(BF)
    S3[...] = dot(TT[0:NP], eye3, 0, 0).astype(BF)
    R3[...] = dot(TT[NP:2 * NP], eye3, 0, 0).astype(BF)
    VF[...] = jnp.zeros_like(VF)
    DN[...] = jnp.zeros_like(DN)

    pl.semaphore_wait(barrier, 1)
    vec_copies = [rdma(vece, VE.at[tp], 0), rdma(vecn, VN.at[tp], 1)]
    for cp in vec_copies:
        cp.start()
    VE[tp] = vece[...]
    VN[tp] = vecn[...]

    loads[0].wait()
    loads[1].wait()
    NF[0] = NST[1].astype(F32)
    node_x = rdma(NF.at[0], NF.at[1], 2)
    node_x.start()

    def wblock(buf, layer, j):
        return buf.at[(layer * 7 + j) // 7, 0 if True else 0]

    def w_pack(layer, j):
        if j == J_NW2:
            half = W2N[layer, tp]
        elif j == J_EW2:
            half = W2E[layer, tp]
        elif j < J_EW2:
            return W1N[layer, j - J_NW1, tp].astype(F32)
        else:
            return W1E[layer, j - J_EW1, tp].astype(F32)
        half = half.astype(F32)
        return cat(half[0:H], half[H:2 * H])

    def w_unpack(layer, j, block):
        block = block.astype(BF)
        if j in (J_NW2, J_EW2):
            ref = W2N if j == J_NW2 else W2E
            ref[layer, ot, 0:H] = block[:, 0:H]
            ref[layer, ot, H:2 * H] = block[:, H:2 * H]
        elif j < J_EW2:
            W1N[layer, j - J_NW1, ot] = block
        else:
            W1E[layer, j - J_EW1, ot] = block

    def w_copy(layer, j):
        return rdma(G.at[1, layer, j], G.at[0, layer, j], 8 + layer * 7 + j)

    def w_send(layer, j):
        G[1, layer, j] = w_pack(layer, j)
        w_copy(layer, j).start()

    def w_recv(layer, j):
        w_copy(layer, j).wait()
        w_unpack(layer, j, G[0, layer, j])

    def lat_copy(b):
        return rdma(HS.at[b, :, 0:H], CS.at[b, :, 0:H], 32 + b)

    def grad_copy(b):
        return rdma(R2.at[b, :, 0:H], R2.at[b, :, H:D], 40 + b)

    loads[2].wait()
    for j in (5, 6, 4):
        w_send(0, j)
    loads[3].wait()
    loads[4].wait()

    def lat_send(b, carry):
        HS[b, :, 0:H] = E1[b, 0].astype(F32)
        lat_copy(b).start()
        return carry

    lax.fori_loop(0, 2, lat_send, 0)
    w_send(0, J_EW2)
    lax.fori_loop(2, NS, lat_send, 0)
    loads[6].wait()
    loads[7].wait()
    for j in (1, 2, 0):
        w_send(0, j)
    for j in (5, 6, 4, 3, 1, 2, 0):
        w_send(1, j)

    loads[8].wait()

    def grad_send(b, carry):
        R2[b, :, 0:H] = E1[b, 1].astype(F32)
        grad_copy(b).start()
        return carry

    lax.fori_loop(0, NS, grad_send, 0)
    loads[10].wait()
    loads[11].wait()
    NF[2] = NST[3].astype(F32)
    node_g = rdma(NF.at[2], NF.at[3], 3)
    node_g.start()

    def node_in(dst, staged, received):
        for b in range(NS):
            own, got = NST[staged, b], NF[received, b].astype(BF)
            lo = jnp.where(tp == 0, own, got)
            hi = jnp.where(tp == 0, got, own)
            dst[b * NP:b * NP + NN] = cat(lo, hi)

    for cp in vec_copies:
        cp.wait()
    node_x.wait()
    node_in(VF.at[0], 0, 1)

    def vec_row(layer, row, node):
        ref = VN if node else VE
        return cat(ref[0, layer, row:row + 1], ref[1, layer, row:row + 1])

    def put3(dst, value):
        parts = split3(value)
        for b in range(NS):
            for k in range(3):
                dst[b, k * NP:(k + 1) * NP] = parts[k][b * NP:(b + 1) * NP]

    def full1(ref, layer, k):
        return ref[layer, k].reshape(D, D)

    def gate(hidden):
        return 0.5 + 0.5 * jnp.tanh(0.5 * hidden)

    def second(act, ref, layer):
        return cat(dot(act, ref[layer, 0]), dot(act, ref[layer, 1]))

    def second_t(dout, ref, layer):
        return dot(dout[:, 0:H], ref[layer, 0], 1, 1) + dot(dout[:, H:D], ref[layer, 1], 1, 1)

    def layer_fwd(layer, src, dst):
        if layer == 0:
            w_recv(0, 5)
            w_recv(0, 6)
        put3(PS, dot(VF[layer], full1(W1E, layer, 1)))
        put3(PR, dot(VF[layer], full1(W1E, layer, 2)))
        if layer == 0:
            w_recv(0, 4)
            w_recv(0, 3)
            loads[5].wait()
        bias = b1e[layer:layer + 1]
        c0, gam, bet = (vec_row(layer, r, False) for r in range(3))

        def edge(b, carry):
            if layer == 0:
                lat_copy(b).wait()
                src[b, ot] = CS[b, :, 0:H].astype(BF)
            lat = cat(src[b, 0], src[b, 1])
            hidden = dot(lat, full1(W1E, layer, 0)) + dot(S3[...], PS[b]) + dot(R3[...], PR[b]) + bias
            HS[b] = hidden
            act = (hidden * gate(hidden)).astype(BF)
            out = second(act, W2E, layer) + c0
            cen = out - mean_cols(out)
            CS[b] = cen
            normed, unused = norm_parts(cen)
            msg = (normed * gam + bet).astype(BF)
            SF[layer, pl.ds(pl.multiple_of(b * NP, NP), NP)] = dot(TT[NP:2 * NP], msg).astype(BF)
            new = (lat.astype(F32) + msg.astype(F32)).astype(BF)
            dst[b, 0] = new[:, 0:H]
            dst[b, 1] = new[:, H:D]
            return carry

        lax.fori_loop(0, NS, edge, 0)
        if layer == 0:
            for cp in spills:
                cp.start()
            for j in (1, 2, 0):
                w_recv(0, j)
        lat = VF[layer]
        hidden = dot(lat, full1(W1N, layer, 0)) + dot(SF[layer], full1(W1N, layer, 1)) + b1n[layer:layer + 1]
        HN[layer] = hidden
        act = (hidden * gate(hidden)).astype(BF)
        out = second(act, W2N, layer) + vec_row(layer, 0, True)
        cen = out - mean_cols(out)
        CN[layer] = cen
        normed, unused = norm_parts(cen)
        msg = (normed * vec_row(layer, 1, True) + vec_row(layer, 2, True)).astype(BF)
        VF[layer + 1] = (lat.astype(F32) + msg.astype(F32)).astype(BF)

    spills = [pltpu.make_async_copy(HS, spill.at[0], spsem.at[0]), pltpu.make_async_copy(CS, spill.at[1], spsem.at[1])]
    fills = [pltpu.make_async_copy(spill.at[0], HS, spsem.at[2]), pltpu.make_async_copy(spill.at[1], CS, spsem.at[3])]

    layer_fwd(0, E0, E1)
    for j in range(7):
        w_recv(1, j)
    loads[9].wait()
    for b in range(NS):
        grad_copy(b).wait()
        DE[b, ot] = R2[b, :, H:D].astype(BF)
    node_g.wait()
    node_in(DN, 2, 3)
    for cp in spills:
        cp.wait()
    layer_fwd(1, E1, E2)

    def put_w2(layer, j, half, value, add):
        if add:
            G[layer, half, j, :, 0:H] += value[0:H]
            G[layer, half, j, :, H:D] += value[H:D]
        else:
            G[layer, half, j, :, 0:H] = value[0:H]
            G[layer, half, j, :, H:D] = value[H:D]

    def put_w1(layer, j, value, add):
        for half in range(2):
            if add:
                G[layer, half, j] += value[half * H:(half + 1) * H]
            else:
                G[layer, half, j] = value[half * H:(half + 1) * H]

    def mlp_bwd(d_msg, cen, hidden, gam, w2, layer, sm, j2, add):
        normed, inv_std = norm_parts(cen)
        sums = [sum_rows(d_msg * normed), sum_rows(d_msg)]
        d_normed = d_msg * gam
        d_out = inv_std * (d_normed - mean_cols(d_normed) - normed * mean_cols(d_normed * normed))
        sums = [sum_rows(d_out)] + sums
        d_out_bf = d_out.astype(BF)
        sig = gate(hidden)
        act = (hidden * sig).astype(BF)
        for half in range(2):
            put_w2(layer, j2, half, dot(act, d_out_bf[:, half * H:(half + 1) * H], 0, 0), add)
        d_hidden = second_t(d_out_bf, w2, layer) * (sig * (1.0 + hidden * (1.0 - sig)))
        sums = [sum_rows(d_hidden)] + sums
        for k in range(4):
            if add:
                SM[sm + k:sm + k + 1] += sums[k]
            else:
                SM[sm + k:sm + k + 1] = sums[k]
        return d_hidden.astype(BF)

    SM[...] = jnp.zeros_like(SM)

    def layer_bwd(layer, src):
        d_node = DN[...].astype(F32)
        d_hid = mlp_bwd(d_node, CN[layer], HN[layer], vec_row(layer, 1, True), W2N, layer, layer * 8, J_NW2, False)
        put_w1(layer, J_NW1, dot(VF[layer], d_hid, 0, 0), False)
        put_w1(layer, J_NW1 + 1, dot(SF[layer], d_hid, 0, 0), False)
        DV[...] = d_node + dot(d_hid, full1(W1N, layer, 0), 1, 1)
        put3(PS, dot(d_hid, full1(W1N, layer, 1), 1, 1))
        for j in (J_EW2, J_EW1):
            G[layer, :, j] = jnp.zeros((2, H, D), F32)
        gam = vec_row(layer, 1, False)
        if layer == 0:
            for cp in fills:
                cp.wait()

        def edge(b, carry):
            d_edge = cat(DE[b, 0], DE[b, 1]).astype(F32)
            d_msg = d_edge + dot(R3[...], PS[b])
            d_hid = mlp_bwd(d_msg, CS[b], HS[b], gam, W2E, layer, layer * 8 + 4, J_EW2, True)
            lat = cat(src[b, 0], src[b, 1])
            put_w1(layer, J_EW1, dot(lat, d_hid, 0, 0), True)
            new = (d_edge + dot(d_hid, full1(W1E, layer, 0), 1, 1)).astype(BF)
            DE[b, 0] = new[:, 0:H]
            DE[b, 1] = new[:, H:D]
            both = dot(TT[...], d_hid).astype(BF)
            at = pl.ds(pl.multiple_of(b * NP, NP), NP)
            GS[at] = both[0:NP]
            GR[at] = both[NP:2 * NP]
            return carry

        lax.fori_loop(0, NS, edge, 0)
        if layer == 1:
            for cp in fills:
                cp.start()
        put_w1(layer, J_EW1 + 1, dot(VF[layer], GS[...], 0, 0), False)
        put_w1(layer, J_EW1 + 2, dot(VF[layer], GR[...], 0, 0), False)
        DN[...] = (DV[...] + dot(GS[...], full1(W1E, layer, 1), 1, 1)
                   + dot(GR[...], full1(W1E, layer, 2), 1, 1)).astype(BF)

    layer_bwd(1, E1)
    layer_bwd(0, E0)

    pl.semaphore_signal(csem, inc=1, device_id=partner, device_id_type=MESH)
    for b in range(NS):
        at = slice(b * NP, b * NP + NN)
        for k, ref in ((0, VF.at[2]), (1, DN)):
            rows = ref[at]
            NST[2 * k, b] = jnp.where(tp == 0, rows[:, 0:H], rows[:, H:D])
            NF[2 * k, b] = jnp.where(tp == 0, rows[:, H:D], rows[:, 0:H]).astype(F32)

    def out_stage(b, carry):
        HS[b, :, 0:H] = E2[b, ot].astype(F32)
        HS[b, :, H:D] = DE[b, ot].astype(F32)
        return carry

    lax.fori_loop(0, NS, out_stage, 0)
    pl.semaphore_wait(csem, 1)
    node_o = [rdma(NF.at[0], NF.at[1], 4), rdma(NF.at[2], NF.at[3], 5)]
    for cp in node_o:
        cp.start()

    def out_copy(b):
        return rdma(HS.at[b], CS.at[b], 48 + b)

    for b in range(NS):
        out_copy(b).start()
    stores = [
        (E2.at[:, tp], o_e.at[mine]), (DE.at[:, tp], o_de.at[mine]),
        (NST.at[0], o_n.at[mine]), (NST.at[2], o_dn.at[mine]),
        (G, o_g), (SM, o_sm),
    ]
    stores = [pltpu.make_async_copy(src, dst, lsem.at[i]) for i, (src, dst) in enumerate(stores)]
    for cp in stores:
        cp.start()
    for k, cp in enumerate(node_o):
        cp.wait()
        NST[2 * k + 1] = NF[2 * k + 1].astype(BF)

    def out_recv(b, carry):
        out_copy(b).wait()
        E1[b, 0] = CS[b, :, 0:H].astype(BF)
        E1[b, 1] = CS[b, :, H:D].astype(BF)
        return carry

    lax.fori_loop(0, NS, out_recv, 0)
    more = [
        (E1.at[:, 0], o_e.at[theirs]), (E1.at[:, 1], o_de.at[theirs]),
        (NST.at[1], o_n.at[theirs]), (NST.at[3], o_dn.at[theirs]),
    ]
    more = [pltpu.make_async_copy(src, dst, lsem.at[6 + i]) for i, (src, dst) in enumerate(more)]
    for cp in more:
        cp.start()
    for cp in stores + more:
        cp.wait()


def compute(*args):
    any_spec = pl.BlockSpec(memory_space=pl.ANY)
    vm = pl.BlockSpec(memory_space=pltpu.VMEM)
    v = pltpu.VMEM
    lat = (2 * NS, NN, H)
    edg = (2 * NS, NE, H)
    outs = [(lat, BF), (edg, BF), (lat, BF), (edg, BF), ((2, 2, 7, H, D), F32), ((16, D), F32), ((2, NS, NE, D), F32)]
    scratch = [
        v((2, 3, 2, H, D), BF), v((2, 2, D, H), BF), v((2, 2, 2, H, D), BF), v((2, 2, D, H), BF),
        v((2, 2, 3, H), F32), v((2, 2, 3, H), F32),
        v((NE, 3 * NP), BF), v((NE, 3 * NP), BF), v((2 * NP, NE), BF),
        v((NS, 2, NE, H), BF), v((NS, 2, NE, H), BF), v((NS, 2, NE, H), BF), v((NS, 2, NE, H), BF),
        v((NS, NE, D), F32), v((NS, NE, D), F32), v((NS, NE, D), F32),
        v((2, 2, 7, H, D), F32), v((NS, 3 * NP, D), BF), v((NS, 3 * NP, D), BF),
        v((4, NS, NN, H), BF), v((4, NS, NN, H), F32),
        v((3, ROWS, D), BF), v((2, ROWS, D), BF), v((2, ROWS, D), F32), v((2, ROWS, D), F32),
        v((ROWS, D), BF), v((ROWS, D), F32), v((ROWS, D), BF), v((ROWS, D), BF), v((16, D), F32),
        pltpu.SemaphoreType.DMA((12,)), pltpu.SemaphoreType.DMA((56,)), pltpu.SemaphoreType.DMA((56,)),
        pltpu.SemaphoreType.REGULAR, pltpu.SemaphoreType.DMA((4,)),
    ]
    return pl.pallas_call(
        body,
        out_shape=[jax.ShapeDtypeStruct(*o) for o in outs],
        in_specs=[any_spec] * 8 + [vm] * 6,
        out_specs=[any_spec] * 7,
        scratch_shapes=scratch,
        compiler_params=pltpu.CompilerParams(
            collective_id=0, has_side_effects=True, vmem_limit_bytes=67043328),
    )(*args)


def solution(mesh):
    lat_spec = P('dp', None, 'tp')
    first_spec = P(None, None, 'tp', None)
    col_spec = P(None, None, 'tp')
    param_specs = (first_spec, P(), col_spec, col_spec, first_spec, P(), col_spec, col_spec)
    in_specs = (lat_spec, lat_spec, P(), P(), lat_spec, lat_spec) + param_specs
    out_specs = (lat_spec, lat_spec, lat_spec, lat_spec) + param_specs

    def local_step(node_lat, edge_lat, senders, receivers, grad_node, grad_edge, edge_w1, edge_b1, edge_w2, edge_vec, node_w1, node_b1, node_w2, node_vec):
        o_n, o_e, o_dn, o_de, grads, small, unused = compute(
            node_lat, edge_lat, grad_node, grad_edge, edge_w1, edge_w2, node_w1, node_w2,
            edge_b1, node_b1, edge_vec, node_vec, senders.reshape(1, NE), receivers.reshape(1, NE))
        grads = lax.psum_scatter(grads, 'tp', scatter_dimension=1, tiled=False)
        grads, small = lax.psum(grads, 'dp'), lax.psum(small, ('dp', 'tp'))
        small = small.reshape(2, 8, D)
        col = lax.axis_index('tp') * H

        def w2(j):
            block = grads[:, j]
            return jnp.concatenate([block[:, :, 0:H], block[:, :, H:D]], axis=1)

        def vec(row):
            return lax.dynamic_slice_in_dim(small[:, row:row + 3], col, H, axis=2)

        return (o_n, o_e, o_dn, o_de,
                grads[:, J_EW1:J_EW1 + 3], small[:, 4], w2(J_EW2), vec(5),
                grads[:, J_NW1:J_NW1 + 2], small[:, 0], w2(J_NW2), vec(1))

    return jax.shard_map(local_step, mesh=mesh, in_specs=in_specs, out_specs=out_specs, check_vma=False)
```

time: 766 us -> 313 us (0.41); the launches traced: 754 us -> 313 us
  other arithmetic: 274 us -> 2.08 us
  matrix products: 132 us -> 0 us
  Pallas kernels: 0 us -> 80.4 us
  waiting for transfers between devices: 198 us -> 156 us
  local copies, waits for them, and re-layouts: 76.9 us -> 36.4 us
  blocking collectives: 56.4 us -> 24.2 us
    scatter-add x6 -> x0, other arithmetic: 164 us -> none  [one_sample(): return jax.ops.segment_sum(sample_rows, seg_ids, num_segments=num_segments)]
    dot_general x42 -> x0, matrix products: 132 us -> none  [the longest x10 29.1 us: mlp_backward(): jnp.einsum('brh,ih->bri', d_hidden_bf, w_first[block_id], preferred_eleme...]
    psum x9 -> x1, waiting for transfers between devices: 198 us -> 112 us  [local_step(): grads, small = (lax.psum(grads, 'dp'), lax.psum(small, ('dp', 'tp')))]
    pallas_call x0 -> x1, Pallas kernels: none -> 80.4 us  [compute(): pl.pallas_call(body, out_shape=[jax.ShapeDtypeStruct(*o) for o in outs],...]
    reduce_sum x15 -> x0, other arithmetic: 63.6 us -> none  [the longest x4 24.5 us: mlp_backward(): jnp.sum(d_hidden, axis=(0, 1))]
    unnamed x9 -> x3, waiting for transfers between devices: 0.15 us -> 43.5 us
    psum x13 -> x1, blocking collectives: 56.4 us -> 24.2 us  [local_step(): grads, small = (lax.psum(grads, 'dp'), lax.psum(small, ('dp', 'tp')))]
    convert_element_type x10 -> x0, other arithmetic: 27.6 us -> none  [the longest x4 16.6 us: mlp_forward(): act_bf = jax.nn.silu(hidden).astype(jnp.bfloat16)]
  transfers between devices with their start and end apart: 9 -> 2, of which waited for: 9 -> 2; matrix products, arithmetic and copies ran while one was open for 17% -> 3% of each run, Pallas kernels for 0% -> 0%
where the time goes in v1:
time: 313 us
  waiting for transfers between devices  156 us (50%)
  Pallas kernels  80.4 us (26%)
  local copies, waits for them, and re-layouts  36.4 us (12%)
  blocking collectives  24.2 us (8%)
  between operations  14.2 us (5%)
    psum x1, waiting for transfers between devices, local_step(): grads, small = (lax.psum(grads, 'dp'), lax.psum(small, ('dp', 'tp')))  112 us
    pallas_call x1, Pallas kernels, compute(): pl.pallas_call(body, out_shape=[jax.ShapeDtypeStruct(*o) for o in outs],...  80.4 us
    unnamed x3, waiting for transfers between devices  43.5 us
    psum x1, blocking collectives, local_step(): grads, small = (lax.psum(grads, 'dp'), lax.psum(small, ('dp', 'tp')))  24.2 us
    unnamed x37, local copies, waits for them, and re-layouts  21 us
    reduce_scatter x1, local copies, waits for them, and re-layouts, local_step(): grads = lax.psum_scatter(grads, 'tp', scatter_dimension=1, tiled=False)  7.65 us
  transfers between devices with their start and end apart: 2, of which 2 were waited for; matrix products, arithmetic and copies ran while one was open for 3% of the time, Pallas kernels for 0%

profile of v1, /device:TPU:0, one launch (start us, length us, event | category | flops | bytes accessed | tf_op | source)
XLA Modules:
  0.0 313.0 jit_solution(7882249115579644175)
XLA Ops:
  7.2 0.0 copy-start.2
  7.2 0.0 all-reduce.6.cloned.1.call-start
  7.2 4.1 %copy.38.el = bf16[16,300,256]{2,1,0:T(8,128)(2,1)} copy(bf16[16,300,256]{2,0,1:T(8,128)(2,1)} %param.15) | data formatting | bytes 4915200 | tf_op args[1]
  11.4 0.0 copy-done.2
  11.4 0.0 copy-start.9
  11.4 0.0 copy-start.10
  11.4 0.0 copy-start.11
  11.4 2.4 copy.40.ge
  13.8 0.0 copy-done.5
  13.8 0.8 copy.37.nl
  14.6 0.0 copy-done.6
  14.6 0.8 copy.39.gn
  15.5 0.0 copy-done.8
  15.5 0.6 copy.41.vece
  16.1 0.0 copy-done.9
  16.1 0.6 copy.42.vecn
  16.7 0.0 copy-done.10
  16.7 0.6 reshape.33.snd
  17.3 0.0 copy-done.11
  17.3 0.6 reshape.34.rcv
  17.8 80.4 %shard_map.229 = (bf16[16,42,256]{2,1,0:T(8,128)(2,1)}, bf16[16,300,256]{2,1,0:T(8,128)(2,1)}, bf16[16,42,256]{2,1,0:T(8,128)(2,1)}, bf16[16,300,256]{2,1,0:T(8,...) custom-call(bf16[16,42,256]{2,1,0:T(8,128)(2,1)} %copy.37.nl, ...), custom_call_target="tpu_custom_call" | custom-call | tf_op jit(solution)/shard_map/pallas_call | solution.py:440
  98.2 0.0 copy-start.12
  98.2 0.0 all-reduce.6.cloned.1.call-update
  98.2 0.0 all-reduce.4.cloned.1.call-start
  98.3 0.6 copy-done.12
  98.9 0.6 dynamic-slice
  99.4 43.5 %all-reduce.6.cloned.1.call-done = f32[2,2,7,256,512]{4,3,2,1,0:T(8,128)} async-done(((f32[2,2,7,256,512]{4,3,2,1,0:T(8,128)}), f32[2,2,7,256,512]{4,3,2,1,0:T(8,128)}) %all-reduce.6.cloned.1.call-update) | async-done | bytes 14680080
  142.9 7.7 %dynamic-slice_bitcast_fusion = f32[2,7,256,512]{3,2,1,0:T(8,128)} fusion(f32[2,2,7,256,512]{4,3,2,1,0:T(8,128)} %all-reduce.6.cloned.1.call-done, u32[]{:T(128)} %bitcast.6), kind=kLoop, calls=%fused_computation | loop fusion | bytes 14680068 | tf_op jit(solution)/shard_map/reduce_scatter | solution.py:463
  150.6 0.0 all-reduce.4.cloned.1.call-update
  150.6 0.7 copy-done.7
  151.4 0.0 copy-start.1
  151.4 4.1 %copy.45 = bf16[16,300,256]{2,0,1:T(8,128)(2,1)} copy(bf16[16,300,256]{2,1,0:T(8,128)(2,1)} %get-tuple-element.37) | data formatting | bytes 4915200
  155.5 0.0 copy-done.1
  155.5 2.3 copy.47
  157.8 0.0 copy-done.4
  157.8 0.8 copy.44
  158.6 0.8 copy.46
  159.5 24.2 %psum.15 = f32[2,8,512]{2,0,1:T(2,128)S(1)} all-reduce(f32[2,8,512]{2,0,1:T(2,128)S(1)} %copy.43), channel_id=1, replica_groups=mesh['dp'=4,'tp'=2] {'dp','tp'}, use_global_device_ids=true, to_apply=%region_2.0 | all-reduce | flops 8192 | bytes 65536 | tf_op jit(solution)/shard_map/psum | solution.py:464
  183.6 0.6 constant_dynamic-slice_fusion
  184.2 0.6 slice_bitcast_fusion.2
  184.8 112.2 %all-reduce.4.cloned.1.call-done = f32[2,7,256,512]{3,2,1,0:T(8,128)} async-done(((f32[2,7,256,512]{3,2,1,0:T(8,128)}), f32[2,7,256,512]{3,2,1,0:T(8,128)}) %all-reduce.4.cloned.1.call-update) | async-done | bytes 7340048 | tf_op jit(solution)/shard_map/psum | solution.py:464
  297.1 1.8 slice_bitcast_fusion
  298.8 0.1 fusion
  299.0 1.0 pad_maximum_fusion.1
  300.0 1.0 pad_maximum_fusion
  301.1 1.6 copy-done
  302.7 2.0 slice.48
  304.6 1.5 slice.54
  (10 shorter events, 0.0 us)
Async XLA Ops:
  7.2 4.2 %copy-start.2 = (bf16[16,300,256]{2,0,1:T(8,128)(2,1)S(1)}, bf16[16,300,256]{2,0,1:T(8,128)(2,1)}, u32[]{:S(2)}) copy-start(bf16[16,300,256]{2,0,1:T(8,128)(2,1)} %param.19) | copy-start | bytes 7372804
  7.2 135.7 %all-reduce.6.cloned.1.call-start = ((), (), s32[]{:S(2)}) async-start(), calls=%async_computation.1 | async-start | bytes 29360128
  11.4 2.4 copy-start.5
  11.4 3.3 %copy-start.6 = (bf16[16,42,256]{2,0,1:T(8,128)(2,1)S(1)}, bf16[16,42,256]{2,0,1:T(8,128)(2,1)}, u32[]{:S(2)}) copy-start(bf16[16,42,256]{2,0,1:T(8,128)(2,1)} %param.18) | copy-start | bytes 1032196
  11.4 4.1 %copy-start.8 = (f32[2,3,256]{2,0,1:T(2,128)S(1)}, f32[2,3,256]{2,0,1:T(2,128)}, u32[]{:S(2)}) copy-start(f32[2,3,256]{2,0,1:T(2,128)} %param.23) | copy-start | bytes 18436
  11.4 4.7 %copy-start.9 = (f32[2,3,256]{2,0,1:T(2,128)S(1)}, f32[2,3,256]{2,0,1:T(2,128)}, u32[]{:S(2)}) copy-start(f32[2,3,256]{2,0,1:T(2,128)} %param.27) | copy-start | bytes 18436
  11.4 5.3 %copy-start.10 = (s32[300]{0:T(512)S(1)}, s32[300]{0:T(512)}, u32[]{:S(2)}) copy-start(s32[300]{0:T(512)} %param.16) | copy-start | bytes 3604
  11.4 5.9 %copy-start.11 = (s32[300]{0:T(512)S(1)}, s32[300]{0:T(512)}, u32[]{:S(2)}) copy-start(s32[300]{0:T(512)} %param.17) | copy-start | bytes 3604
  98.2 0.7 copy-start.12
  98.2 198.8 %all-reduce.4.cloned.1.call-start = ((), (), s32[]{:S(2)}) async-start(), calls=%async_computation | async-start | bytes 14680064 | tf_op jit(solution)/shard_map/psum | solution.py:464
  150.6 0.8 copy-start.7
  151.4 4.2 %copy-start.1 = (bf16[16,300,256]{2,1,0:T(8,128)(2,1)S(1)}, bf16[16,300,256]{2,1,0:T(8,128)(2,1)}, u32[]{:S(2)}) copy-start(bf16[16,300,256]{2,1,0:T(8,128)(2,1)} %get-tuple-element.39) | copy-start | bytes 7372804
  155.5 2.3 copy-start.4
  155.5 3.1 copy-start.3
  298.8 3.8 %copy-start = (f32[2,7,256,512]{3,2,1,0:T(8,128)S(1)}, f32[2,7,256,512]{3,2,1,0:T(8,128)}, u32[]{:S(2)}) copy-start(f32[2,7,256,512]{3,2,1,0:T(8,128)} %all-reduce.4.cloned.1.call-done) | copy-start | bytes 22020100
Sparse Core Ops, SparseCore 0:
  98.4 44.5 all-reduce.5
  150.7 146.3 all-reduce.3

commit v2 on v1

v2 whole, which is shorter than its diff:
```python
import functools

import jax
import jax.numpy as jnp
from jax import lax
from jax.experimental import pallas as pl
from jax.experimental.pallas import tpu as pltpu
from jax.sharding import PartitionSpec as P

BF = jnp.bfloat16
F32 = jnp.float32
MESH = pl.DeviceIdType.MESH
LN_EPS = 1e-5
NS = 8
NN = 42
NE = 300
D = 512
H = 256
ROWS = NN * NS
NB = 10
BE = NE // NB
BR = BE * NS


def dot(lhs, rhs, lc=1, rc=0):
    return lax.dot_general(lhs, rhs, (((lc,), (rc,)), ((), ())), preferred_element_type=F32)


def cat(lhs, rhs):
    return jnp.concatenate([lhs, rhs], axis=1)


def mean_cols(x):
    return jnp.sum(x, axis=1, keepdims=True) * (1.0 / D)


def sum_rows(x):
    return jnp.sum(x, axis=0, keepdims=True)


def norm_parts(centered):
    inv_std = lax.rsqrt(mean_cols(centered * centered) + LN_EPS)
    return centered * inv_std, inv_std


J_NW2, J_NW1, J_EW2, J_EW1 = 0, 1, 3, 4


def rows_of(block):
    return block.astype(F32).reshape(block.shape[0] * NS, block.shape[2])


def body(nl, el, gn, ge, w1e, w2e, w1n, w2n, b1e, b1n, vece, vecn, flat, snd, rcv,
         o_n, o_e, o_dn, o_de, o_g, o_sm, spill,
         W1E, W2E, W1N, W2N, VE, VN, KS, KR,
         E0, E1, E2, DE, HS, CS, R2, G, PS, PR, GA, AG,
         NST, NF, VF, SF, HN, CN, DN, DV, SM,
         lsem, ssem, rsem, csem, spsem):
    dp = lax.axis_index('dp')
    tp = lax.axis_index('tp')
    ot = 1 - tp
    partner = (dp, ot)

    def rdma(src, dst, idx):
        return pltpu.make_async_remote_copy(
            src_ref=src, dst_ref=dst, send_sem=ssem.at[idx], recv_sem=rsem.at[idx],
            device_id=partner, device_id_type=MESH)

    mine = pl.ds(pl.multiple_of(tp * NS, NS), NS)
    theirs = pl.ds(pl.multiple_of(ot * NS, NS), NS)
    loads = [
        (nl.at[:, mine], NST.at[0]), (nl.at[:, theirs], NST.at[1]),
        (w1e, W1E.at[:, :, tp]), (el.at[:, theirs], E1.at[0]), (w2e, W2E.at[:, tp]),
        (el.at[:, mine], E0.at[tp]), (w1n, W1N.at[:, :, tp]), (w2n, W2N.at[:, tp]),
        (ge.at[:, theirs], E1.at[1]), (ge.at[:, mine], DE.at[tp]),
        (gn.at[:, mine], NST.at[2]), (gn.at[:, theirs], NST.at[3]),
    ]
    loads = [pltpu.make_async_copy(src, dst, lsem.at[i]) for i, (src, dst) in enumerate(loads)]
    for cp in loads:
        cp.start()

    barrier = pltpu.get_barrier_semaphore()
    pl.semaphore_signal(barrier, inc=1, device_id=partner, device_id_type=MESH)

    pl.semaphore_wait(barrier, 1)
    vec_copies = [rdma(vece, VE.at[tp], 0), rdma(vecn, VN.at[tp], 1)]
    for cp in vec_copies:
        cp.start()
    VE[tp] = vece[...]
    VN[tp] = vecn[...]

    loads[0].wait()
    loads[1].wait()
    NF[0] = NST[1].astype(F32)
    node_x = rdma(NF.at[0], NF.at[1], 2)
    node_x.start()

    def w_pack(layer, j):
        if j == J_NW2:
            half = W2N[layer, tp]
        elif j == J_EW2:
            half = W2E[layer, tp]
        elif j < J_EW2:
            return W1N[layer, j - J_NW1, tp].astype(F32)
        else:
            return W1E[layer, j - J_EW1, tp].astype(F32)
        half = half.astype(F32)
        return cat(half[0:H], half[H:2 * H])

    def w_unpack(layer, j, block):
        block = block.astype(BF)
        if j in (J_NW2, J_EW2):
            ref = W2N if j == J_NW2 else W2E
            ref[layer, ot, 0:H] = block[:, 0:H]
            ref[layer, ot, H:2 * H] = block[:, H:2 * H]
        elif j < J_EW2:
            W1N[layer, j - J_NW1, ot] = block
        else:
            W1E[layer, j - J_EW1, ot] = block

    def w_copy(layer, j):
        return rdma(G.at[1, layer, j], G.at[0, layer, j], 8 + layer * 7 + j)

    def w_send(layer, j):
        G[1, layer, j] = w_pack(layer, j)
        w_copy(layer, j).start()

    def w_recv(layer, j):
        w_copy(layer, j).wait()
        w_unpack(layer, j, G[0, layer, j])

    def edges(b):
        return pl.ds(b * BE, BE)

    def erows(b):
        return pl.ds(pl.multiple_of(b * BR, BR), BR)

    def lat_copy(b):
        return rdma(HS.at[erows(b), 0:H], CS.at[erows(b), 0:H], 24 + b)

    def grad_copy(b):
        return rdma(R2.at[erows(b), 0:H], R2.at[erows(b), H:D], 34 + b)

    loads[2].wait()
    for j in (5, 6, 4):
        w_send(0, j)
    loads[3].wait()
    loads[4].wait()

    def lat_send(b, carry):
        HS[erows(b), 0:H] = rows_of(E1[0, edges(b)])
        lat_copy(b).start()
        return carry

    lat_send(0, 0)
    w_send(0, J_EW2)
    lax.fori_loop(1, NB, lat_send, 0)
    loads[6].wait()
    loads[7].wait()
    for j in (1, 2, 0):
        w_send(0, j)
    for j in (5, 6, 4, 3, 1, 2, 0):
        w_send(1, j)

    loads[8].wait()

    def grad_send(b, carry):
        R2[erows(b), 0:H] = rows_of(E1[1, edges(b)])
        grad_copy(b).start()
        return carry

    lax.fori_loop(0, NB, grad_send, 0)
    loads[10].wait()
    loads[11].wait()
    NF[2] = NST[3].astype(F32)
    node_g = rdma(NF.at[2], NF.at[3], 3)
    node_g.start()

    def select(dst, base):
        def one(b, carry):
            rows = lax.broadcasted_iota(jnp.int32, (ROWS, BR), 0)
            dst[b] = jnp.where(rows == flat[base + b], 1.0, 0.0).astype(BF)
            return carry
        lax.fori_loop(0, NB, one, 0)

    select(KR, NB)
    select(KS, 0)

    def node_in(dst, staged, received):
        own, got = rows_of(NST[staged]), rows_of(NF[received])
        lo = jnp.where(tp == 0, own, got)
        hi = jnp.where(tp == 0, got, own)
        dst[...] = cat(lo, hi).astype(BF)

    for cp in vec_copies:
        cp.wait()
    node_x.wait()
    node_in(VF.at[0], 0, 1)

    def vec_row(layer, row, node):
        ref = VN if node else VE
        return cat(ref[0, row, layer:layer + 1], ref[1, row, layer:layer + 1])

    def full1(ref, layer, k):
        return ref[layer, k].reshape(D, D)

    def gate(hidden):
        return 0.5 + 0.5 * jnp.tanh(0.5 * hidden)

    def second(act, ref, layer):
        return cat(dot(act, ref[layer, 0]), dot(act, ref[layer, 1]))

    def second_t(dout, ref, layer):
        return dot(dout[:, 0:H], ref[layer, 0], 1, 1) + dot(dout[:, H:D], ref[layer, 1], 1, 1)

    def layer_fwd(layer, src, dst):
        if layer == 0:
            w_recv(0, 5)
            w_recv(0, 6)
        PS[...] = (dot(VF[layer], full1(W1E, layer, 1)) + b1e[layer:layer + 1]).reshape(NN, NS, D)
        PR[...] = dot(VF[layer], full1(W1E, layer, 2)).reshape(NN, NS, D)
        if layer == 0:
            w_recv(0, 4)
            w_recv(0, 3)
            loads[5].wait()
        c0, gam, bet = (vec_row(layer, r, False) for r in range(3))
        AG[...] = jnp.zeros_like(AG)

        def edge(b, carry):
            if layer == 0:
                lat_copy(b).wait()
                src[ot, edges(b)] = CS[erows(b), 0:H].reshape(BE, NS, H).astype(BF)
            for i in range(BE):
                GA[i * NS:(i + 1) * NS] = PS[snd[b * BE + i]] + PR[rcv[b * BE + i]]
            lat = cat(rows_of(src[0, edges(b)]), rows_of(src[1, edges(b)]))
            hidden = dot(lat.astype(BF), full1(W1E, layer, 0)) + GA[...]
            HS[erows(b)] = hidden
            act = (hidden * gate(hidden)).astype(BF)
            out = second(act, W2E, layer) + c0
            cen = out - mean_cols(out)
            CS[erows(b)] = cen
            normed, unused = norm_parts(cen)
            msg = (normed * gam + bet).astype(BF)
            AG[...] += dot(KR[b], msg)
            new = lat + msg.astype(F32)
            dst[0, edges(b)] = new[:, 0:H].reshape(BE, NS, H).astype(BF)
            dst[1, edges(b)] = new[:, H:D].reshape(BE, NS, H).astype(BF)
            return carry

        lax.fori_loop(0, NB, edge, 0)
        if layer == 0:
            for cp in spills:
                cp.start()
            for j in (1, 2, 0):
                w_recv(0, j)
        SF[layer] = AG[...].astype(BF)
        lat = VF[layer]
        hidden = dot(lat, full1(W1N, layer, 0)) + dot(SF[layer], full1(W1N, layer, 1)) + b1n[layer:layer + 1]
        HN[layer] = hidden
        act = (hidden * gate(hidden)).astype(BF)
        out = second(act, W2N, layer) + vec_row(layer, 0, True)
        cen = out - mean_cols(out)
        CN[layer] = cen
        normed, unused = norm_parts(cen)
        msg = (normed * vec_row(layer, 1, True) + vec_row(layer, 2, True)).astype(BF)
        VF[layer + 1] = (lat.astype(F32) + msg.astype(F32)).astype(BF)

    spills = [pltpu.make_async_copy(HS, spill.at[0], spsem.at[0]), pltpu.make_async_copy(CS, spill.at[1], spsem.at[1])]
    fills = [pltpu.make_async_copy(spill.at[0], HS, spsem.at[2]), pltpu.make_async_copy(spill.at[1], CS, spsem.at[3])]

    layer_fwd(0, E0, E1)
    for j in range(7):
        w_recv(1, j)
    loads[9].wait()

    def grad_recv(b, carry):
        grad_copy(b).wait()
        DE[ot, edges(b)] = R2[erows(b), H:D].reshape(BE, NS, H).astype(BF)
        return carry

    lax.fori_loop(0, NB, grad_recv, 0)
    node_g.wait()
    node_in(DN, 2, 3)
    for cp in spills:
        cp.wait()
    layer_fwd(1, E1, E2)

    def put_w2(layer, j, half, value, add):
        if add:
            G[layer, half, j, :, 0:H] += value[0:H]
            G[layer, half, j, :, H:D] += value[H:D]
        else:
            G[layer, half, j, :, 0:H] = value[0:H]
            G[layer, half, j, :, H:D] = value[H:D]

    def put_w1(layer, j, value, add):
        for half in range(2):
            if add:
                G[layer, half, j] += value[half * H:(half + 1) * H]
            else:
                G[layer, half, j] = value[half * H:(half + 1) * H]

    def mlp_bwd(d_msg, cen, hidden, gam, w2, layer, sm, j2, add):
        normed, inv_std = norm_parts(cen)
        sums = [sum_rows(d_msg * normed), sum_rows(d_msg)]
        d_normed = d_msg * gam
        d_out = inv_std * (d_normed - mean_cols(d_normed) - normed * mean_cols(d_normed * normed))
        sums = [sum_rows(d_out)] + sums
        d_out_bf = d_out.astype(BF)
        sig = gate(hidden)
        act = (hidden * sig).astype(BF)
        for half in range(2):
            put_w2(layer, j2, half, dot(act, d_out_bf[:, half * H:(half + 1) * H], 0, 0), add)
        d_hidden = second_t(d_out_bf, w2, layer) * (sig * (1.0 + hidden * (1.0 - sig)))
        sums = [sum_rows(d_hidden)] + sums
        for k in range(4):
            if add:
                SM[sm + k:sm + k + 1] += sums[k]
            else:
                SM[sm + k:sm + k + 1] = sums[k]
        return d_hidden.astype(BF)

    SM[...] = jnp.zeros_like(SM)

    def layer_bwd(layer, src):
        d_node = DN[...].astype(F32)
        d_hid = mlp_bwd(d_node, CN[layer], HN[layer], vec_row(layer, 1, True), W2N, layer, layer * 8, J_NW2, False)
        put_w1(layer, J_NW1, dot(VF[layer], d_hid, 0, 0), False)
        put_w1(layer, J_NW1 + 1, dot(SF[layer], d_hid, 0, 0), False)
        DV[...] = d_node + dot(d_hid, full1(W1N, layer, 0), 1, 1)
        PS[...] = dot(d_hid, full1(W1N, layer, 1), 1, 1).reshape(NN, NS, D)
        for j in (J_EW2, J_EW1):
            G[layer, :, j] = jnp.zeros((2, H, D), F32)
        AG[...] = jnp.zeros_like(AG)
        PR[...] = jnp.zeros_like(PR)
        gam = vec_row(layer, 1, False)
        if layer == 0:
            for cp in fills:
                cp.wait()

        def edge(b, carry):
            for i in range(BE):
                GA[i * NS:(i + 1) * NS] = PS[rcv[b * BE + i]]
            d_edge = cat(rows_of(DE[0, edges(b)]), rows_of(DE[1, edges(b)]))
            d_hid = mlp_bwd(d_edge + GA[...], CS[erows(b)], HS[erows(b)], gam, W2E, layer, layer * 8 + 4, J_EW2, True)
            lat = cat(rows_of(src[0, edges(b)]), rows_of(src[1, edges(b)])).astype(BF)
            put_w1(layer, J_EW1, dot(lat, d_hid, 0, 0), True)
            new = d_edge + dot(d_hid, full1(W1E, layer, 0), 1, 1)
            DE[0, edges(b)] = new[:, 0:H].reshape(BE, NS, H).astype(BF)
            DE[1, edges(b)] = new[:, H:D].reshape(BE, NS, H).astype(BF)
            AG[...] += dot(KS[b], d_hid)
            PR[...] += dot(KR[b], d_hid).reshape(NN, NS, D)
            return carry

        lax.fori_loop(0, NB, edge, 0)
        if layer == 1:
            for cp in fills:
                cp.start()
        d_ps, d_pr = AG[...].astype(BF), rows_of(PR[...]).astype(BF)
        put_w1(layer, J_EW1 + 1, dot(VF[layer], d_ps, 0, 0), False)
        put_w1(layer, J_EW1 + 2, dot(VF[layer], d_pr, 0, 0), False)
        DN[...] = (DV[...] + dot(d_ps, full1(W1E, layer, 1), 1, 1)
                   + dot(d_pr, full1(W1E, layer, 2), 1, 1)).astype(BF)

    layer_bwd(1, E1)
    layer_bwd(0, E0)

    pl.semaphore_signal(csem, inc=1, device_id=partner, device_id_type=MESH)
    for k, ref in ((0, VF.at[2]), (1, DN)):
        rows = ref[...].astype(F32)
        NST[2 * k] = jnp.where(tp == 0, rows[:, 0:H], rows[:, H:D]).reshape(NN, NS, H).astype(BF)
        NF[2 * k] = jnp.where(tp == 0, rows[:, H:D], rows[:, 0:H]).reshape(NN, NS, H)

    def out_stage(b, carry):
        HS[erows(b), 0:H] = rows_of(E2[ot, edges(b)])
        HS[erows(b), H:D] = rows_of(DE[ot, edges(b)])
        return carry

    lax.fori_loop(0, NB, out_stage, 0)
    pl.semaphore_wait(csem, 1)
    node_o = [rdma(NF.at[0], NF.at[1], 4), rdma(NF.at[2], NF.at[3], 5)]
    for cp in node_o:
        cp.start()

    def out_copy(b):
        return rdma(HS.at[erows(b)], CS.at[erows(b)], 44 + b)

    for b in range(NB):
        out_copy(b).start()
    stores = [
        (E2.at[tp], o_e.at[:, mine]), (DE.at[tp], o_de.at[:, mine]),
        (NST.at[0], o_n.at[:, mine]), (NST.at[2], o_dn.at[:, mine]),
        (G, o_g), (SM, o_sm),
    ]
    stores = [pltpu.make_async_copy(src, dst, lsem.at[i]) for i, (src, dst) in enumerate(stores)]
    for cp in stores:
        cp.start()
    for k, cp in enumerate(node_o):
        cp.wait()
        NST[2 * k + 1] = NF[2 * k + 1].astype(BF)

    def out_recv(b, carry):
        out_copy(b).wait()
        E1[0, edges(b)] = CS[erows(b), 0:H].reshape(BE, NS, H).astype(BF)
        E1[1, edges(b)] = CS[erows(b), H:D].reshape(BE, NS, H).astype(BF)
        return carry

    lax.fori_loop(0, NB, out_recv, 0)
    more = [
        (E1.at[0], o_e.at[:, theirs]), (E1.at[1], o_de.at[:, theirs]),
        (NST.at[1], o_n.at[:, theirs]), (NST.at[3], o_dn.at[:, theirs]),
    ]
    more = [pltpu.make_async_copy(src, dst, lsem.at[6 + i]) for i, (src, dst) in enumerate(more)]
    for cp in more:
        cp.start()
    for cp in stores + more:
        cp.wait()


def compute(*args):
    any_spec = pl.BlockSpec(memory_space=pl.ANY)
    vm = pl.BlockSpec(memory_space=pltpu.VMEM)
    sm = pl.BlockSpec(memory_space=pltpu.SMEM)
    v = pltpu.VMEM
    lat = (NN, 2 * NS, H)
    edg = (NE, 2 * NS, H)
    outs = [(lat, BF), (edg, BF), (lat, BF), (edg, BF), ((2, 2, 7, H, D), F32), ((16, D), F32), ((2, NE * NS, D), F32)]
    scratch = [
        v((2, 3, 2, H, D), BF), v((2, 2, D, H), BF), v((2, 2, 2, H, D), BF), v((2, 2, D, H), BF),
        v((2, 3, 2, H), F32), v((2, 3, 2, H), F32),
        v((NB, ROWS, BR), BF), v((NB, ROWS, BR), BF),
        v((2, NE, NS, H), BF), v((2, NE, NS, H), BF), v((2, NE, NS, H), BF), v((2, NE, NS, H), BF),
        v((NE * NS, D), F32), v((NE * NS, D), F32), v((NE * NS, D), F32),
        v((2, 2, 7, H, D), F32), v((NN, NS, D), F32), v((NN, NS, D), F32), v((BR, D), F32), v((ROWS, D), F32),
        v((4, NN, NS, H), BF), v((4, NN, NS, H), F32),
        v((3, ROWS, D), BF), v((2, ROWS, D), BF), v((2, ROWS, D), F32), v((2, ROWS, D), F32),
        v((ROWS, D), BF), v((ROWS, D), F32), v((16, D), F32),
        pltpu.SemaphoreType.DMA((12,)), pltpu.SemaphoreType.DMA((56,)), pltpu.SemaphoreType.DMA((56,)),
        pltpu.SemaphoreType.REGULAR, pltpu.SemaphoreType.DMA((4,)),
    ]
    return pl.pallas_call(
        body,
        out_shape=[jax.ShapeDtypeStruct(*o) for o in outs],
        in_specs=[any_spec] * 8 + [vm] * 5 + [sm] * 2,
        out_specs=[any_spec] * 7,
        scratch_shapes=scratch,
        compiler_params=pltpu.CompilerParams(
            collective_id=0, has_side_effects=True, vmem_limit_bytes=67043328),
    )(*args)


def solution(mesh):
    lat_spec = P('dp', None, 'tp')
    first_spec = P(None, None, 'tp', None)
    col_spec = P(None, None, 'tp')
    param_specs = (first_spec, P(), col_spec, col_spec, first_spec, P(), col_spec, col_spec)
    in_specs = (lat_spec, lat_spec, P(), P(), lat_spec, lat_spec) + param_specs
    out_specs = (lat_spec, lat_spec, lat_spec, lat_spec) + param_specs

    def local_step(node_lat, edge_lat, senders, receivers, grad_node, grad_edge, edge_w1, edge_b1, edge_w2, edge_vec, node_w1, node_b1, node_w2, node_vec):
        def swap(x):
            return jnp.transpose(x, (1, 0, 2))

        ids = jnp.stack([senders, receivers])
        flat = ids[:, :, None] * NS + jnp.arange(NS, dtype=jnp.int32)
        o_n, o_e, o_dn, o_de, grads, small, unused = compute(
            swap(node_lat), swap(edge_lat), swap(grad_node), swap(grad_edge), edge_w1, edge_w2, node_w1, node_w2,
            edge_b1, node_b1, swap(edge_vec), swap(node_vec), flat.reshape(2 * NB, 1, BR), senders, receivers)
        o_n, o_e, o_dn, o_de = swap(o_n), swap(o_e), swap(o_dn), swap(o_de)
        grads = lax.psum_scatter(grads, 'tp', scatter_dimension=1, tiled=False)
        grads, small = lax.psum(grads, 'dp'), lax.psum(small, ('dp', 'tp'))
        small = small.reshape(2, 8, D)
        col = lax.axis_index('tp') * H

        def w2(j):
            block = grads[:, j]
            return jnp.concatenate([block[:, :, 0:H], block[:, :, H:D]], axis=1)

        def vec(row):
            return lax.dynamic_slice_in_dim(small[:, row:row + 3], col, H, axis=2)

        return (o_n, o_e, o_dn, o_de,
                grads[:, J_EW1:J_EW1 + 3], small[:, 4], w2(J_EW2), vec(5),
                grads[:, J_NW1:J_NW1 + 2], small[:, 0], w2(J_NW2), vec(1))

    return jax.shard_map(local_step, mesh=mesh, in_specs=in_specs, out_specs=out_specs, check_vma=False)
```

time: 313 us -> 311 us (level)
  local copies, waits for them, and re-layouts: 36.4 us -> 24.7 us
  waiting for transfers between devices: 156 us -> 164 us
    unnamed x37 -> x19, local copies, waits for them, and re-layouts: 21 us -> 8.31 us
    psum x1, waiting for transfers between devices: 112 us -> 120 us  [local_step(): grads, small = (lax.psum(grads, 'dp'), lax.psum(small, ('dp', 'tp')))]
  transfers between devices with their start and end apart: 2 -> 2, of which waited for: 2 -> 2; matrix products, arithmetic and copies ran while one was open for 3% -> 1% of each run, Pallas kernels for 0% -> 0%
where the time goes in v2:
time: 311 us
  waiting for transfers between devices  164 us (53%)
  Pallas kernels  81.8 us (26%)
  local copies, waits for them, and re-layouts  24.7 us (8%)
  blocking collectives  24.2 us (8%)
  between operations  14.1 us (5%)
    psum x1, waiting for transfers between devices, local_step(): grads, small = (lax.psum(grads, 'dp'), lax.psum(small, ('dp', 'tp')))  120 us
    pallas_call x1, Pallas kernels, compute(): pl.pallas_call(body, out_shape=[jax.ShapeDtypeStruct(*o) for o in outs],...  81.8 us
    unnamed x3, waiting for transfers between devices  43.5 us
    psum x1, blocking collectives, local_step(): grads, small = (lax.psum(grads, 'dp'), lax.psum(small, ('dp', 'tp')))  24.2 us
    unnamed x19, local copies, waits for them, and re-layouts  8.31 us
    reduce_scatter x1, local copies, waits for them, and re-layouts, local_step(): grads = lax.psum_scatter(grads, 'tp', scatter_dimension=1, tiled=False)  7.64 us
  transfers between devices with their start and end apart: 2, of which 2 were waited for; matrix products, arithmetic and copies ran while one was open for 1% of the time, Pallas kernels for 0%

profile of v2, /device:TPU:0, one launch (start us, length us, event | category | flops | bytes accessed | tf_op | source)
XLA Modules:
  0.0 310.8 jit_solution(11748270575842141169)
XLA Ops:
  7.2 0.0 all-reduce.6.cloned.1.call-start
  7.2 0.7 stack.10
  7.9 0.7 stack.9
  8.6 0.1 iota_add_fusion
  8.8 0.8 add.40.flat
  9.6 81.8 %shard_map.229 = (bf16[42,16,256]{2,1,0:T(8,128)(2,1)}, bf16[300,16,256]{2,1,0:T(8,128)(2,1)}, bf16[42,16,256]{2,1,0:T(8,128)(2,1)}, bf16[300,16,256]{2,1,0:T(8,...) custom-call(bf16[42,16,256]{2,1,0:T(8,128)(2,1)} %bitcast.32, ...), custom_call_target="tpu_custom_call" | custom-call | tf_op jit(solution)/shard_map/pallas_call | solution.py:441
  91.3 0.0 copy-start.6
  91.3 0.0 all-reduce.6.cloned.1.call-update
  91.4 0.0 all-reduce.4.cloned.1.call-start
  91.4 0.6 copy-done.6
  92.0 0.6 dynamic-slice
  92.6 43.5 %all-reduce.6.cloned.1.call-done = f32[2,2,7,256,512]{4,3,2,1,0:T(8,128)} async-done(((f32[2,2,7,256,512]{4,3,2,1,0:T(8,128)}), f32[2,2,7,256,512]{4,3,2,1,0:T(8,128)}) %all-reduce.6.cloned.1.call-update) | async-done | bytes 14680080
  136.0 7.6 %dynamic-slice_bitcast_fusion = f32[2,7,256,512]{3,2,1,0:T(8,128)} fusion(f32[2,2,7,256,512]{4,3,2,1,0:T(8,128)} %all-reduce.6.cloned.1.call-done, u32[]{:T(128)} %bitcast.16), kind=kLoop, calls=%fused_computation | loop fusion | bytes 14680068 | tf_op jit(solution)/shard_map/reduce_scatter | solution.py:470
  143.7 0.0 copy-start.5
  143.7 0.0 all-reduce.4.cloned.1.call-update
  143.7 0.7 copy-done.5
  144.5 24.2 %psum.15 = f32[2,8,512]{2,0,1:T(2,128)S(1)} all-reduce(f32[2,8,512]{2,0,1:T(2,128)S(1)} %copy.30), channel_id=1, replica_groups=mesh['dp'=4,'tp'=2] {'dp','tp'}, use_global_device_ids=true, to_apply=%region_2.0 | all-reduce | flops 8192 | bytes 65536 | tf_op jit(solution)/shard_map/psum | solution.py:471
  168.7 0.6 constant_dynamic-slice_fusion
  169.3 0.6 slice_bitcast_fusion.2
  169.9 120.2 %all-reduce.4.cloned.1.call-done = f32[2,7,256,512]{3,2,1,0:T(8,128)} async-done(((f32[2,7,256,512]{3,2,1,0:T(8,128)}), f32[2,7,256,512]{3,2,1,0:T(8,128)}) %all-reduce.4.cloned.1.call-update) | async-done | bytes 7340048 | tf_op jit(solution)/shard_map/psum | solution.py:471
  290.1 1.8 slice_bitcast_fusion
  291.9 0.0 copy-start
  291.9 0.1 fusion
  292.0 1.0 pad_maximum_fusion.1
  293.1 1.0 pad_maximum_fusion
  294.1 1.6 copy-done
  295.7 2.0 slice.48
  297.7 0.0 copy-start.4
  297.7 0.0 copy-start.2
  297.7 1.5 slice.54
  299.2 0.0 copy-start.3
  299.2 0.0 copy-done.4
  299.2 0.0 copy-start.1
  299.2 0.7 copy.39
  299.9 0.5 copy-done.2
  300.4 1.4 copy.40
  301.8 0.0 copy-done.3
  301.8 0.7 copy.41
  302.5 0.0 copy-done.1
  302.6 1.4 copy.42
  (3 shorter events, 0.0 us)
Async XLA Ops:
  7.2 128.9 %all-reduce.6.cloned.1.call-start = ((), (), s32[]{:S(2)}) async-start(), calls=%async_computation.1 | async-start | bytes 29360128
  91.3 0.7 copy-start.6
  91.4 198.7 %all-reduce.4.cloned.1.call-start = ((), (), s32[]{:S(2)}) async-start(), calls=%async_computation | async-start | bytes 14680064 | tf_op jit(solution)/shard_map/psum | solution.py:471
  143.7 0.8 copy-start.5
  291.9 3.8 %copy-start = (f32[2,7,256,512]{3,2,1,0:T(8,128)S(1)}, f32[2,7,256,512]{3,2,1,0:T(8,128)}, u32[]{:S(2)}) copy-start(f32[2,7,256,512]{3,2,1,0:T(8,128)} %all-reduce.4.cloned.1.call-done) | copy-start | bytes 22020100
  297.7 1.5 copy-start.4
  297.7 2.7 copy-start.2
  299.2 2.6 copy-start.3
  299.2 3.4 %copy-start.1 = (bf16[300,16,256]{2,1,0:T(8,128)(2,1)S(1)}, bf16[300,16,256]{2,1,0:T(8,128)(2,1)}, u32[]{:S(2)}) copy-start(bf16[300,16,256]{2,1,0:T(8,128)(2,1)} %get-tuple-element.21) | copy-start | bytes 7372804
Sparse Core Ops, SparseCore 0:
  91.5 44.5 all-reduce.5
  143.8 146.2 all-reduce.3

commit v3 on v2

--- a/solution.py
+++ b/solution.py
@@ -26,6 +26,14 @@
     return lax.dot_general(lhs, rhs, (((lc,), (rc,)), ((), ())), preferred_element_type=F32)
 
 
+def dot_rows(lhs, rhs):
+    return dot(lhs, rhs, 0, 0)
+
+
+def dot_cols(lhs, rhs):
+    return dot(lhs, rhs, 1, 1)
+
+
 def cat(lhs, rhs):
     return jnp.concatenate([lhs, rhs], axis=1)
 
@@ -51,15 +59,19 @@
 
 
 def body(nl, el, gn, ge, w1e, w2e, w1n, w2n, b1e, b1n, vece, vecn, flat, snd, rcv,
-         o_n, o_e, o_dn, o_de, o_g, o_sm, spill,
+         o_n, o_e, o_dn, o_de, o_ew1, o_ew2, o_nw1, o_nw2, o_be, o_bn, o_ve, o_vn, spill,
          W1E, W2E, W1N, W2N, VE, VN, KS, KR,
          E0, E1, E2, DE, HS, CS, R2, G, PS, PR, GA, AG,
          NST, NF, VF, SF, HN, CN, DN, DV, SM,
-         lsem, ssem, rsem, csem, spsem):
+         lsem, ssem, rsem, csem, spsem, gssem, grsem, osem):
     dp = lax.axis_index('dp')
     tp = lax.axis_index('tp')
     ot = 1 - tp
     partner = (dp, ot)
+    cx, cy = lax.rem(dp, 2), dp // 2
+    x_peer = (cy * 2 + 1 - cx, tp)
+    y_peer = ((1 - cy) * 2 + cx, tp)
+    peers = (partner, x_peer, y_peer)
 
     def rdma(src, dst, idx):
         return pltpu.make_async_remote_copy(
@@ -80,9 +92,9 @@
         cp.start()
 
     barrier = pltpu.get_barrier_semaphore()
-    pl.semaphore_signal(barrier, inc=1, device_id=partner, device_id_type=MESH)
-
-    pl.semaphore_wait(barrier, 1)
+    for peer in peers:
+        pl.semaphore_signal(barrier, inc=1, device_id=peer, device_id_type=MESH)
+    pl.semaphore_wait(barrier, 3)
     vec_copies = [rdma(vece, VE.at[tp], 0), rdma(vecn, VN.at[tp], 1)]
     for cp in vec_copies:
         cp.start()
@@ -105,14 +117,14 @@
         else:
             return W1E[layer, j - J_EW1, tp].astype(F32)
         half = half.astype(F32)
-        return cat(half[0:H], half[H:2 * H])
+        return cat(half[:H], half[H:])
 
     def w_unpack(layer, j, block):
         block = block.astype(BF)
         if j in (J_NW2, J_EW2):
             ref = W2N if j == J_NW2 else W2E
-            ref[layer, ot, 0:H] = block[:, 0:H]
-            ref[layer, ot, H:2 * H] = block[:, H:2 * H]
+            ref[layer, ot, :H] = block[:, :H]
+            ref[layer, ot, H:] = block[:, H:]
         elif j < J_EW2:
             W1N[layer, j - J_NW1, ot] = block
         else:
@@ -136,10 +148,10 @@
         return pl.ds(pl.multiple_of(b * BR, BR), BR)
 
     def lat_copy(b):
-        return rdma(HS.at[erows(b), 0:H], CS.at[erows(b), 0:H], 24 + b)
+        return rdma(HS.at[erows(b), :H], CS.at[erows(b), :H], 24 + b)
 
     def grad_copy(b):
-        return rdma(R2.at[erows(b), 0:H], R2.at[erows(b), H:D], 34 + b)
+        return rdma(R2.at[erows(b), :H], R2.at[erows(b), H:], 34 + b)
 
     loads[2].wait()
     for j in (5, 6, 4):
@@ -148,7 +160,7 @@
     loads[4].wait()
 
     def lat_send(b, carry):
-        HS[erows(b), 0:H] = rows_of(E1[0, edges(b)])
+        HS[erows(b), :H] = rows_of(E1[0, edges(b)])
         lat_copy(b).start()
         return carry
 
@@ -165,7 +177,7 @@
     loads[8].wait()
 
     def grad_send(b, carry):
-        R2[erows(b), 0:H] = rows_of(E1[1, edges(b)])
+        R2[erows(b), :H] = rows_of(E1[1, edges(b)])
         grad_copy(b).start()
         return carry
 
@@ -211,7 +223,7 @@
         return cat(dot(act, ref[layer, 0]), dot(act, ref[layer, 1]))
 
     def second_t(dout, ref, layer):
-        return dot(dout[:, 0:H], ref[layer, 0], 1, 1) + dot(dout[:, H:D], ref[layer, 1], 1, 1)
+        return dot_cols(dout[:, :H], ref[layer, 0]) + dot_cols(dout[:, H:], ref[layer, 1])
 
     def layer_fwd(layer, src, dst):
         if layer == 0:
@@ -229,7 +241,7 @@
         def edge(b, carry):
             if layer == 0:
                 lat_copy(b).wait()
-                src[ot, edges(b)] = CS[erows(b), 0:H].reshape(BE, NS, H).astype(BF)
+                src[ot, edges(b)] = CS[erows(b), :H].reshape(BE, NS, H).astype(BF)
             for i in range(BE):
                 GA[i * NS:(i + 1) * NS] = PS[snd[b * BE + i]] + PR[rcv[b * BE + i]]
             lat = cat(rows_of(src[0, edges(b)]), rows_of(src[1, edges(b)]))
@@ -243,8 +255,8 @@
             msg = (normed * gam + bet).astype(BF)
             AG[...] += dot(KR[b], msg)
             new = lat + msg.astype(F32)
-            dst[0, edges(b)] = new[:, 0:H].reshape(BE, NS, H).astype(BF)
-            dst[1, edges(b)] = new[:, H:D].reshape(BE, NS, H).astype(BF)
+            dst[0, edges(b)] = new[:, :H].reshape(BE, NS, H).astype(BF)
+            dst[1, edges(b)] = new[:, H:].reshape(BE, NS, H).astype(BF)
             return carry
 
         lax.fori_loop(0, NB, edge, 0)
@@ -275,23 +287,131 @@
 
     def grad_recv(b, carry):
         grad_copy(b).wait()
-        DE[ot, edges(b)] = R2[erows(b), H:D].reshape(BE, NS, H).astype(BF)
+        DE[ot, edges(b)] = R2[erows(b), H:].reshape(BE, NS, H).astype(BF)
         return carry
 
     lax.fori_loop(0, NB, grad_recv, 0)
+    for peer in peers:
+        pl.semaphore_signal(csem.at[0], inc=1, device_id=peer, device_id_type=MESH)
     node_g.wait()
     node_in(DN, 2, 3)
     for cp in spills:
         cp.wait()
     layer_fwd(1, E1, E2)
 
+    def chunk(c):
+        return 1 - c // 7, c % 7
+
+    def g_copy(c, k, src, dst, peer):
+        return pltpu.make_async_remote_copy(
+            src_ref=src, dst_ref=dst, send_sem=gssem.at[c, k], recv_sem=grsem.at[c, k],
+            device_id=peer, device_id_type=MESH)
+
+    def core_copy(c):
+        layer, j = chunk(c)
+        return g_copy(c, 0, G.at[layer, ot, j], R2.at[j * H:(j + 1) * H], partner)
+
+    def landing(c):
+        layer, j = chunk(c)
+        if layer == 1:
+            return lambda lo, n: R2.at[7 * H + j * 192 + lo:7 * H + j * 192 + lo + n]
+        return lambda lo, n: G.at[1, tp, j, lo:lo + n]
+
+    half_p, half_q = cx * 64, 128 + cy * 64
+    quarter_p, quarter_q = half_p + cy * 32, half_q + cx * 32
+
+    def strip(c, start, n, final=False):
+        layer, j = chunk(c)
+        return G.at[layer, ot if final else tp, j, pl.ds(pl.multiple_of(start, 32), n)]
+
+    def a_copies(c):
+        land = landing(c)
+        return [g_copy(c, 1, strip(c, 64 - half_p, 64), land(0, 64), x_peer),
+                g_copy(c, 2, strip(c, 320 - half_q, 64), land(64, 64), y_peer)]
+
+    def b_copies(c):
+        land = landing(c)
+        return [g_copy(c, 3, strip(c, half_p + 32 - cy * 32, 32), land(128, 32), y_peer),
+                g_copy(c, 4, strip(c, half_q + 32 - cx * 32, 32), land(160, 32), x_peer)]
+
+    def c_copies(c):
+        ref_p, ref_q = strip(c, quarter_p, 32, True), strip(c, quarter_q, 32, True)
+        return [g_copy(c, 5, ref_p, ref_p, y_peer), g_copy(c, 6, ref_q, ref_q, x_peer)]
+
+    def d_copies(c):
+        ref_p, ref_q = strip(c, half_p, 64, True), strip(c, half_q, 64, True)
+        return [g_copy(c, 7, ref_p, ref_p, x_peer), g_copy(c, 8, ref_q, ref_q, y_peer)]
+
+    def store_copies(c):
+        layer, j = chunk(c)
+        src = G.at[layer, ot, j]
+        if j in (J_NW2, J_EW2):
+            ref = o_nw2 if j == J_NW2 else o_ew2
+            pairs = [(src.at[:, :H], ref.at[layer, :H]), (src.at[:, H:], ref.at[layer, H:])]
+        elif j < J_EW2:
+            pairs = [(src, o_nw1.at[layer, j - J_NW1])]
+        else:
+            pairs = [(src, o_ew1.at[layer, j - J_EW1])]
+        return [pltpu.make_async_copy(a, b, osem.at[c, k]) for k, (a, b) in enumerate(pairs)]
+
+    def wait_all(copies):
+        for cp in copies:
+            cp.wait()
+
+    def start_all(copies):
+        for cp in copies:
+            cp.start()
+
+    def stage0(c):
+        core_copy(c).start()
+
+    def stage1(c):
+        layer, j = chunk(c)
+        core_copy(c).wait()
+        G[layer, tp, j] += R2[j * H:(j + 1) * H]
+        start_all(a_copies(c))
+
+    def stage2(c):
+        land = landing(c)
+        wait_all(a_copies(c))
+        for start, lo in ((half_p, 0), (half_q, 64)):
+            ref = strip(c, start, 64)
+            ref[...] += land(lo, 64)[...]
+        start_all(b_copies(c))
+
+    def stage3(c):
+        land = landing(c)
+        wait_all(b_copies(c))
+        for start, lo in ((quarter_p, 128), (quarter_q, 160)):
+            strip(c, start, 32, True)[...] = strip(c, start, 32)[...] + land(lo, 32)[...]
+        start_all(c_copies(c))
+
+    def stage4(c):
+        wait_all(c_copies(c))
+        start_all(d_copies(c))
+
+    def stage5(c):
+        wait_all(d_copies(c))
+        start_all(store_copies(c))
+
+    def run(stage, chunks):
+        for c in chunks:
+            stage(c)
+
+    node1, edge1, node0, edge0 = (list(range(*ends)) for ends in ((0, 3), (3, 7), (7, 10), (10, 14)))
+
+    plan = {
+        1: [(stage1, node1, 0), (stage2, node1, 4), (stage3, node1, 7)],
+        0: [(stage5, node1, 0), (stage2, edge1, 1), (stage1, node0, 5), (stage3, edge1, 5), (stage4, edge1[:2], 8)],
+    }
+
     def put_w2(layer, j, half, value, add):
         if add:
-            G[layer, half, j, :, 0:H] += value[0:H]
-            G[layer, half, j, :, H:D] += value[H:D]
+            G[layer, half, j, :, :H] += value[:H]
+            G[layer, half, j, :, H:] += value[H:]
         else:
-            G[layer, half, j, :, 0:H] = value[0:H]
-            G[layer, half, j, :, H:D] = value[H:D]
+            G[layer, half, j, :, :H] = value[:H]
+            G[layer, half, j, :, H:] = value[H:]
 
     def put_w1(layer, j, value, add):
         for half in range(2):
@@ -310,14 +430,14 @@
         sig = gate(hidden)
         act = (hidden * sig).astype(BF)
         for half in range(2):
-            put_w2(layer, j2, half, dot(act, d_out_bf[:, half * H:(half + 1) * H], 0, 0), add)
+            put_w2(layer, j2, half, dot_rows(act, d_out_bf[:, half * H:(half + 1) * H]), add)
         d_hidden = second_t(d_out_bf, w2, layer) * (sig * (1.0 + hidden * (1.0 - sig)))
         sums = [sum_rows(d_hidden)] + sums
         for k in range(4):
             if add:
-                SM[sm + k:sm + k + 1] += sums[k]
+                SM[0, sm + k:sm + k + 1] += sums[k]
             else:
-                SM[sm + k:sm + k + 1] = sums[k]
+                SM[0, sm + k:sm + k + 1] = sums[k]
         return d_hidden.astype(BF)
 
     SM[...] = jnp.zeros_like(SM)
@@ -325,10 +445,15 @@
     def layer_bwd(layer, src):
         d_node = DN[...].astype(F32)
         d_hid = mlp_bwd(d_node, CN[layer], HN[layer], vec_row(layer, 1, True), W2N, layer, layer * 8, J_NW2, False)
-        put_w1(layer, J_NW1, dot(VF[layer], d_hid, 0, 0), False)
-        put_w1(layer, J_NW1 + 1, dot(SF[layer], d_hid, 0, 0), False)
-        DV[...] = d_node + dot(d_hid, full1(W1N, layer, 0), 1, 1)
-        PS[...] = dot(d_hid, full1(W1N, layer, 1), 1, 1).reshape(NN, NS, D)
+        nodes, edge_w2, edge_w1 = (node1, edge1[:1], edge1[1:]) if layer else (node0, edge0[:1], edge0[1:])
+        pl.semaphore_wait(csem.at[1 - layer], 3 if layer == 1 else 1)
+        stage0(nodes[0])
+        put_w1(layer, J_NW1, dot_rows(VF[layer], d_hid), False)
+        stage0(nodes[1])
+        put_w1(layer, J_NW1 + 1, dot_rows(SF[layer], d_hid), False)
+        stage0(nodes[2])
+        DV[...] = d_node + dot_cols(d_hid, full1(W1N, layer, 0))
+        PS[...] = dot_cols(d_hid, full1(W1N, layer, 1)).reshape(NN, NS, D)
         for j in (J_EW2, J_EW1):
             G[layer, :, j] = jnp.zeros((2, H, D), F32)
         AG[...] = jnp.zeros_like(AG)
@@ -344,40 +469,54 @@
             d_edge = cat(rows_of(DE[0, edges(b)]), rows_of(DE[1, edges(b)]))
             d_hid = mlp_bwd(d_edge + GA[...], CS[erows(b)], HS[erows(b)], gam, W2E, layer, layer * 8 + 4, J_EW2, True)
             lat = cat(rows_of(src[0, edges(b)]), rows_of(src[1, edges(b)])).astype(BF)
-            put_w1(layer, J_EW1, dot(lat, d_hid, 0, 0), True)
-            new = d_edge + dot(d_hid, full1(W1E, layer, 0), 1, 1)
-            DE[0, edges(b)] = new[:, 0:H].reshape(BE, NS, H).astype(BF)
-            DE[1, edges(b)] = new[:, H:D].reshape(BE, NS, H).astype(BF)
+            put_w1(layer, J_EW1, dot_rows(lat, d_hid), True)
+            new = d_edge + dot_cols(d_hid, full1(W1E, layer, 0))
+            DE[0, edges(b)] = new[:, :H].reshape(BE, NS, H).astype(BF)
+            DE[1, edges(b)] = new[:, H:].reshape(BE, NS, H).astype(BF)
             AG[...] += dot(KS[b], d_hid)
             PR[...] += dot(KR[b], d_hid).reshape(NN, NS, D)
+            for stage, chunks, first in plan[layer]:
+                for i, c in enumerate(chunks):
+                    pl.when(b == first + i)(functools.partial(stage, c))
             return carry
 
         lax.fori_loop(0, NB, edge, 0)
         if layer == 1:
             for cp in fills:
                 cp.start()
+        run(stage0, edge_w2 + edge_w1[:1])
         d_ps, d_pr = AG[...].astype(BF), rows_of(PR[...]).astype(BF)
-        put_w1(layer, J_EW1 + 1, dot(VF[layer], d_ps, 0, 0), False)
-        put_w1(layer, J_EW1 + 2, dot(VF[layer], d_pr, 0, 0), False)
-        DN[...] = (DV[...] + dot(d_ps, full1(W1E, layer, 1), 1, 1)
-                   + dot(d_pr, full1(W1E, layer, 2), 1, 1)).astype(BF)
+        put_w1(layer, J_EW1 + 1, dot_rows(VF[layer], d_ps), False)
+        stage0(edge_w1[1])
+        put_w1(layer, J_EW1 + 2, dot_rows(VF[layer], d_pr), False)
+        stage0(edge_w1[2])
+        DN[...] = (DV[...] + dot_cols(d_ps, full1(W1E, layer, 1))
+                   + dot_cols(d_pr, full1(W1E, layer, 2))).astype(BF)
 
     layer_bwd(1, E1)
+    run(stage1, edge1)
+    run(stage4, node1)
+    pl.semaphore_signal(csem.at[1], inc=1, device_id=partner, device_id_type=MESH)
     layer_bwd(0, E0)
-
-    pl.semaphore_signal(csem, inc=1, device_id=partner, device_id_type=MESH)
+    run(stage4, edge1[2:])
+    run(stage1, edge0)
+
+    pl.semaphore_signal(csem.at[2], inc=1, device_id=partner, device_id_type=MESH)
+    run(stage2, node0)
     for k, ref in ((0, VF.at[2]), (1, DN)):
         rows = ref[...].astype(F32)
-        NST[2 * k] = jnp.where(tp == 0, rows[:, 0:H], rows[:, H:D]).reshape(NN, NS, H).astype(BF)
-        NF[2 * k] = jnp.where(tp == 0, rows[:, H:D], rows[:, 0:H]).reshape(NN, NS, H)
+        NST[2 * k] = jnp.where(tp == 0, rows[:, :H], rows[:, H:]).reshape(NN, NS, H).astype(BF)
+        NF[2 * k] = jnp.where(tp == 0, rows[:, H:], rows[:, :H]).reshape(NN, NS, H)
 
     def out_stage(b, carry):
-        HS[erows(b), 0:H] = rows_of(E2[ot, edges(b)])
-        HS[erows(b), H:D] = rows_of(DE[ot, edges(b)])
+        HS[erows(b), :H] = rows_of(E2[ot, edges(b)])
+        HS[erows(b), H:] = rows_of(DE[ot, edges(b)])
         return carry
 
     lax.fori_loop(0, NB, out_stage, 0)
-    pl.semaphore_wait(csem, 1)
+    pl.semaphore_wait(csem.at[2], 1)
+    small0 = rdma(SM.at[0], SM.at[1], 6)
+    small0.start()
     node_o = [rdma(NF.at[0], NF.at[1], 4), rdma(NF.at[2], NF.at[3], 5)]
     for cp in node_o:
         cp.start()
@@ -390,8 +529,8 @@
     stores = [
         (E2.at[tp], o_e.at[:, mine]), (DE.at[tp], o_de.at[:, mine]),
         (NST.at[0], o_n.at[:, mine]), (NST.at[2], o_dn.at[:, mine]),
-        (G, o_g), (SM, o_sm),
     ]
+    run(stage5, edge1)
     stores = [pltpu.make_async_copy(src, dst, lsem.at[i]) for i, (src, dst) in enumerate(stores)]
     for cp in stores:
         cp.start()
@@ -401,10 +540,11 @@
 
     def out_recv(b, carry):
         out_copy(b).wait()
-        E1[0, edges(b)] = CS[erows(b), 0:H].reshape(BE, NS, H).astype(BF)
-        E1[1, edges(b)] = CS[erows(b), H:D].reshape(BE, NS, H).astype(BF)
+        E1[0, edges(b)] = CS[erows(b), :H].reshape(BE, NS, H).astype(BF)
+        E1[1, edges(b)] = CS[erows(b), H:].reshape(BE, NS, H).astype(BF)
         return carry
 
+    run(stage3, node0)
     lax.fori_loop(0, NB, out_recv, 0)
     more = [
         (E1.at[0], o_e.at[:, theirs]), (E1.at[1], o_de.at[:, theirs]),
@@ -413,6 +553,34 @@
     more = [pltpu.make_async_copy(src, dst, lsem.at[6 + i]) for i, (src, dst) in enumerate(more)]
     for cp in more:
         cp.start()
+    small0.wait()
+    SM[2] = SM[0] + SM[1]
+    small1 = pltpu.make_async_remote_copy(
+        src_ref=SM.at[2], dst_ref=SM.at[3], send_sem=ssem.at[7], recv_sem=rsem.at[7],
+        device_id=x_peer, device_id_type=MESH)
+    small1.start()
+    run(stage2, edge0)
+    run(stage4, node0)
+    small1.wait()
+    SM[4] = SM[2] + SM[3]
+    small2 = pltpu.make_async_remote_copy(
+        src_ref=SM.at[4], dst_ref=SM.at[5], send_sem=ssem.at[54], recv_sem=rsem.at[54],
+        device_id=y_peer, device_id_type=MESH)
+    small2.start()
+    run(stage3, edge0)
+    small2.wait()
+    total = SM[4] + SM[5]
+    for layer in range(2):
+        for row, ref_b, ref_v in ((0, o_bn, o_vn), (4, o_be, o_ve)):
+            at = layer * 8 + row
+            ref_b[layer:layer + 1] = total[at:at + 1]
+            for k in range(3):
+                one = total[at + 1 + k:at + 2 + k]
+                ref_v[k, layer:layer + 1] = jnp.where(tp == 0, one[:, :H], one[:, H:])
+    run(stage4, edge0)
+    run(stage5, node0 + edge0)
+    for c in node1 + edge1 + node0 + edge0:
+        wait_all(store_copies(c))
     for cp in stores + more:
         cp.wait()
 
@@ -424,25 +592,27 @@
     v = pltpu.VMEM
     lat = (NN, 2 * NS, H)
     edg = (NE, 2 * NS, H)
-    outs = [(lat, BF), (edg, BF), (lat, BF), (edg, BF), ((2, 2, 7, H, D), F32), ((16, D), F32), ((2, NE * NS, D), F32)]
+    outs = [(lat, BF), (edg, BF), (lat, BF), (edg, BF),
+            ((2, 3, H, D), F32), ((2, D, H), F32), ((2, 2, H, D), F32), ((2, D, H), F32),
+            ((2, D), F32), ((2, D), F32), ((3, 2, H), F32), ((3, 2, H), F32), ((2, NE * NS, D), F32)]
+    dma = pltpu.SemaphoreType.DMA
+    node = (ROWS, D)
     scratch = [
         v((2, 3, 2, H, D), BF), v((2, 2, D, H), BF), v((2, 2, 2, H, D), BF), v((2, 2, D, H), BF),
-        v((2, 3, 2, H), F32), v((2, 3, 2, H), F32),
-        v((NB, ROWS, BR), BF), v((NB, ROWS, BR), BF),
-        v((2, NE, NS, H), BF), v((2, NE, NS, H), BF), v((2, NE, NS, H), BF), v((2, NE, NS, H), BF),
-        v((NE * NS, D), F32), v((NE * NS, D), F32), v((NE * NS, D), F32),
-        v((2, 2, 7, H, D), F32), v((NN, NS, D), F32), v((NN, NS, D), F32), v((BR, D), F32), v((ROWS, D), F32),
+        *[v((2, 3, 2, H), F32)] * 2, *[v((NB, ROWS, BR), BF)] * 2, *[v((2, NE, NS, H), BF)] * 4,
+        v((NE * NS, D), F32), v((NE * NS, D), F32), v((7 * (H + 192), D), F32), v((2, 2, 7, H, D), F32),
+        v((NN, NS, D), F32), v((NN, NS, D), F32), v((BR, D), F32), v(node, F32),
         v((4, NN, NS, H), BF), v((4, NN, NS, H), F32),
-        v((3, ROWS, D), BF), v((2, ROWS, D), BF), v((2, ROWS, D), F32), v((2, ROWS, D), F32),
-        v((ROWS, D), BF), v((ROWS, D), F32), v((16, D), F32),
-        pltpu.SemaphoreType.DMA((12,)), pltpu.SemaphoreType.DMA((56,)), pltpu.SemaphoreType.DMA((56,)),
-        pltpu.SemaphoreType.REGULAR, pltpu.SemaphoreType.DMA((4,)),
+        v((3, *node), BF), v((2, *node), BF), v((2, *node), F32), v((2, *node), F32),
+        v(node, BF), v(node, F32), v((6, 16, D), F32),
+        dma((12,)), dma((56,)), dma((56,)), pltpu.SemaphoreType.REGULAR((3,)), dma((4,)),
+        dma((14, 9)), dma((14, 9)), dma((14, 2)),
     ]
     return pl.pallas_call(
         body,
         out_shape=[jax.ShapeDtypeStruct(*o) for o in outs],
         in_specs=[any_spec] * 8 + [vm] * 5 + [sm] * 2,
-        out_specs=[any_spec] * 7,
+        out_specs=[any_spec] * 8 + [vm] * 4 + [any_spec],
         scratch_shapes=scratch,
         compiler_params=pltpu.CompilerParams(
             collective_id=0, has_side_effects=True, vmem_limit_bytes=67043328),
@@ -463,24 +633,10 @@
 
         ids = jnp.stack([senders, receivers])
         flat = ids[:, :, None] * NS + jnp.arange(NS, dtype=jnp.int32)
-        o_n, o_e, o_dn, o_de, grads, small, unused = compute(
+        outs = compute(
             swap(node_lat), swap(edge_lat), swap(grad_node), swap(grad_edge), edge_w1, edge_w2, node_w1, node_w2,
             edge_b1, node_b1, swap(edge_vec), swap(node_vec), flat.reshape(2 * NB, 1, BR), senders, receivers)
-        o_n, o_e, o_dn, o_de = swap(o_n), swap(o_e), swap(o_dn), swap(o_de)
-        grads = lax.psum_scatter(grads, 'tp', scatter_dimension=1, tiled=False)
-        grads, small = lax.psum(grads, 'dp'), lax.psum(small, ('dp', 'tp'))
-        small = small.reshape(2, 8, D)
-        col = lax.axis_index('tp') * H
-
-        def w2(j):
-            block = grads[:, j]
-            return jnp.concatenate([block[:, :, 0:H], block[:, :, H:D]], axis=1)
-
-        def vec(row):
-            return lax.dynamic_slice_in_dim(small[:, row:row + 3], col, H, axis=2)
-
-        return (o_n, o_e, o_dn, o_de,
-                grads[:, J_EW1:J_EW1 + 3], small[:, 4], w2(J_EW2), vec(5),
-                grads[:, J_NW1:J_NW1 + 2], small[:, 0], w2(J_NW2), vec(1))
+        o_ew1, o_ew2, o_nw1, o_nw2, o_be, o_bn, o_ve, o_vn = outs[4:12]
+        return tuple(swap(x) for x in outs[:4]) + (o_ew1, o_be, o_ew2, swap(o_ve), o_nw1, o_bn, o_nw2, swap(o_vn))
 
     return jax.shard_map(local_step, mesh=mesh, in_specs=in_specs, out_specs=out_specs, check_vma=False)

time: 311 us -> 187 us (0.60)
  waiting for transfers between devices: 164 us -> 0 us
  Pallas kernels: 81.8 us -> 167 us
  blocking collectives: 24.2 us -> 0 us
  between operations: 14.1 us -> 0.68 us
  local copies, waits for them, and re-layouts: 24.7 us -> 18.2 us
    psum x1 -> x0, waiting for transfers between devices: 120 us -> none  [local_step(): grads, small = (lax.psum(grads, 'dp'), lax.psum(small, ('dp', 'tp')))]
    pallas_call x1, Pallas kernels: 81.8 us -> 167 us  [compute(): pl.pallas_call(body, out_shape=[jax.ShapeDtypeStruct(*o) for o in outs],...]
    unnamed x3 -> x0, waiting for transfers between devices: 43.5 us -> none
    psum x1 -> x0, blocking collectives: 24.2 us -> none  [local_step(): grads, small = (lax.psum(grads, 'dp'), lax.psum(small, ('dp', 'tp')))]
    unnamed x19 -> x32, local copies, waits for them, and re-layouts: 8.31 us -> 16 us
    reduce_scatter x1 -> x0, local copies, waits for them, and re-layouts: 7.64 us -> none  [local_step(): grads = lax.psum_scatter(grads, 'tp', scatter_dimension=1, tiled=False)]
    slice x4 -> x0, local copies, waits for them, and re-layouts: 3.6 us -> none  [the longest x1 1.97 us: local_step(): grads[:, J_EW1:J_EW1 + 3]]
  transfers between devices with their start and end apart: 2 -> 0, of which waited for: 2 -> 0; matrix products, arithmetic and copies ran while one was open for 1% -> 0% of each run, Pallas kernels for 0% -> 0%
where the time goes in v3:
time: 187 us; the launch traced here: 186 us
  Pallas kernels  167 us (89%)
  local copies, waits for them, and re-layouts  18.2 us (10%)
    pallas_call x1, Pallas kernels, compute(): pl.pallas_call(body, out_shape=[jax.ShapeDtypeStruct(*o) for o in outs],...  167 us
    unnamed x32, local copies, waits for them, and re-layouts  16 us

profile of v3, /device:TPU:0, one launch (start us, length us, event | category | flops | bytes accessed | tf_op | source)
XLA Modules:
  0.0 186.2 jit_solution(8441486261796876667)
XLA Ops:
  0.6 0.7 stack.9
  1.3 0.7 stack.10
  2.0 0.1 iota_add_fusion
  2.2 0.8 add.27.flat
  3.0 167.2 %shard_map.229 = (bf16[42,16,256]{2,1,0:T(8,128)(2,1)}, bf16[300,16,256]{2,1,0:T(8,128)(2,1)}, bf16[42,16,256]{2,1,0:T(8,128)(2,1)}, bf16[300,16,256]{2,1,0:T(8,...) custom-call(bf16[42,16,256]{2,1,0:T(8,128)(2,1)} %bitcast.16, ...), custom_call_target="tpu_custom_call" | custom-call | tf_op jit(solution)/shard_map/pallas_call | solution.py:611
  170.2 1.7 copy.39
  171.9 0.0 copy-start.5
  171.9 0.0 copy-start.1
  171.9 3.4 %copy.40 = bf16[16,300,256]{2,0,1:T(8,128)(2,1)} copy(bf16[16,300,256]{2,0,1:T(8,128)(2,1)} %bitcast.15) | data formatting | bytes 4915200
  175.4 0.0 copy-done.5
  175.4 0.7 copy.41
  176.1 0.0 copy-done.1
  176.1 0.0 copy-start
  176.1 1.4 copy.42
  177.6 1.3 copy-done
  178.9 0.0 copy-start.9
  178.9 0.0 copy-start.4
  178.9 0.0 copy-start.7
  178.9 1.7 copy.43
  180.6 0.0 copy-done.9
  180.6 0.0 copy-start.2
  180.6 0.6 copy.44
  181.2 0.0 copy-done.4
  181.2 1.0 copy.45
  182.1 0.0 copy-done.7
  182.1 0.0 copy-start.8
  182.1 0.0 copy-start.3
  182.1 0.6 copy.46
  182.7 0.0 copy-done.2
  182.7 0.0 copy-start.6
  182.7 1.3 copy.47
  184.1 0.0 copy-done.8
  184.1 0.6 copy.48
  184.7 0.0 copy-done.3
  184.7 1.0 copy.49
  185.6 0.0 copy-done.6
  185.6 0.6 copy.50
  (1 shorter events, 0.0 us)
Async XLA Ops:
  171.9 3.4 %copy-start.5 = (bf16[42,16,256]{2,1,0:T(8,128)(2,1)S(1)}, bf16[42,16,256]{2,1,0:T(8,128)(2,1)}, u32[]{:S(2)}) copy-start(bf16[42,16,256]{2,1,0:T(8,128)(2,1)} %get-tuple-element.26) | copy-start | bytes 1032196
  171.9 4.2 %copy-start.1 = (bf16[300,16,256]{2,1,0:T(8,128)(2,1)S(1)}, bf16[300,16,256]{2,1,0:T(8,128)(2,1)}, u32[]{:S(2)}) copy-start(bf16[300,16,256]{2,1,0:T(8,128)(2,1)} %get-tuple-element.27) | copy-start | bytes 7372804
  176.1 2.8 %copy-start = (f32[2,3,256,512]{3,2,1,0:T(8,128)S(1)}, f32[2,3,256,512]{3,2,1,0:T(8,128)}, u32[]{:S(2)}) copy-start(f32[2,3,256,512]{3,2,1,0:T(8,128)} %get-tuple-element.52) | copy-start | bytes 9437188
  178.9 1.7 copy-start.9
  178.9 2.3 %copy-start.4 = (f32[2,512,256]{2,1,0:T(8,128)S(1)}, f32[2,512,256]{2,1,0:T(8,128)}, u32[]{:S(2)}) copy-start(f32[2,512,256]{2,1,0:T(8,128)} %get-tuple-element.54) | copy-start | bytes 3145732
  178.9 3.2 %copy-start.7 = (f32[3,2,256]{2,1,0:T(2,128)S(1)}, f32[3,2,256]{2,1,0:T(2,128)}, u32[]{:S(2)}) copy-start(f32[3,2,256]{2,1,0:T(2,128)} %get-tuple-element.31) | copy-start | bytes 18436
  180.6 2.2 %copy-start.2 = (f32[2,2,256,512]{3,2,1,0:T(8,128)S(1)}, f32[2,2,256,512]{3,2,1,0:T(8,128)}, u32[]{:S(2)}) copy-start(f32[2,2,256,512]{3,2,1,0:T(8,128)} %get-tuple-element.56) | copy-start | bytes 6291460
  182.1 1.9 %copy-start.8 = (f32[2,512]{1,0:T(2,128)S(1)}, f32[2,512]{1,0:T(2,128)}, u32[]{:S(2)}) copy-start(f32[2,512]{1,0:T(2,128)} %get-tuple-element.57) | copy-start | bytes 12292
  182.1 2.5 %copy-start.3 = (f32[2,512,256]{2,1,0:T(8,128)S(1)}, f32[2,512,256]{2,1,0:T(8,128)}, u32[]{:S(2)}) copy-start(f32[2,512,256]{2,1,0:T(8,128)} %get-tuple-element.58) | copy-start | bytes 3145732
  182.7 2.9 %copy-start.6 = (f32[3,2,256]{2,1,0:T(2,128)S(1)}, f32[3,2,256]{2,1,0:T(2,128)}, u32[]{:S(2)}) copy-start(f32[3,2,256]{2,1,0:T(2,128)} %get-tuple-element.35) | copy-start | bytes 18436

commit v4 on v3

--- a/solution.py
+++ b/solution.py
@@ -58,7 +58,7 @@
     return block.astype(F32).reshape(block.shape[0] * NS, block.shape[2])
 
 
-def body(nl, el, gn, ge, w1e, w2e, w1n, w2n, b1e, b1n, vece, vecn, flat, snd, rcv,
+def body(nl, el, gn, ge, w1e, w2e, w1n, w2n, b1e, b1n, vece, vecn, snd, rcv,
          o_n, o_e, o_dn, o_de, o_ew1, o_ew2, o_nw1, o_nw2, o_be, o_bn, o_ve, o_vn, spill,
          W1E, W2E, W1N, W2N, VE, VN, KS, KR,
          E0, E1, E2, DE, HS, CS, R2, G, PS, PR, GA, AG,
@@ -73,10 +73,18 @@
     y_peer = ((1 - cy) * 2 + cx, tp)
     peers = (partner, x_peer, y_peer)
 
-    def rdma(src, dst, idx):
+    def rdma(src, dst, idx, peer=None):
         return pltpu.make_async_remote_copy(
             src_ref=src, dst_ref=dst, send_sem=ssem.at[idx], recv_sem=rsem.at[idx],
-            device_id=partner, device_id_type=MESH)
+            device_id=peer or partner, device_id_type=MESH)
+
+    def wait_all(copies):
+        for cp in copies:
+            cp.wait()
+
+    def start_all(copies):
+        for cp in copies:
+            cp.start()
 
     mine = pl.ds(pl.multiple_of(tp * NS, NS), NS)
     theirs = pl.ds(pl.multiple_of(ot * NS, NS), NS)
@@ -94,6 +102,9 @@
     barrier = pltpu.get_barrier_semaphore()
     for peer in peers:
         pl.semaphore_signal(barrier, inc=1, device_id=peer, device_id_type=MESH)
+    loads[0].wait()
+    loads[1].wait()
+    NF[0] = NST[1].astype(F32)
     pl.semaphore_wait(barrier, 3)
     vec_copies = [rdma(vece, VE.at[tp], 0), rdma(vecn, VN.at[tp], 1)]
     for cp in vec_copies:
@@ -101,9 +112,6 @@
     VE[tp] = vece[...]
     VN[tp] = vecn[...]
 
-    loads[0].wait()
-    loads[1].wait()
-    NF[0] = NST[1].astype(F32)
     node_x = rdma(NF.at[0], NF.at[1], 2)
     node_x.start()
 
@@ -130,16 +138,20 @@
         else:
             W1E[layer, j - J_EW1, ot] = block
 
-    def w_copy(layer, j):
-        return rdma(G.at[1, layer, j], G.at[0, layer, j], 8 + layer * 7 + j)
-
-    def w_send(layer, j):
-        G[1, layer, j] = w_pack(layer, j)
-        w_copy(layer, j).start()
-
-    def w_recv(layer, j):
-        w_copy(layer, j).wait()
-        w_unpack(layer, j, G[0, layer, j])
+    groups = [(0, J_EW1 + 1, 2), (0, J_EW1, 1), (0, J_EW2, 1), (0, 0, 3), (1, 0, 7)]
+    w_copies = [rdma(G.at[1, layer, pl.ds(lo, n)], G.at[0, layer, pl.ds(lo, n)], 8 + k)
+                for k, (layer, lo, n) in enumerate(groups)]
+
+    def w_packs(k):
+        layer, lo, n = groups[k]
+        for j in range(lo, lo + n):
+            G[1, layer, j] = w_pack(layer, j)
+
+    def w_recv(k):
+        layer, lo, n = groups[k]
+        w_copies[k].wait()
+        for j in range(lo, lo + n):
+            w_unpack(layer, j, G[0, layer, j])
 
     def edges(b):
         return pl.ds(b * BE, BE)
@@ -147,56 +159,42 @@
     def erows(b):
         return pl.ds(pl.multiple_of(b * BR, BR), BR)
 
-    def lat_copy(b):
-        return rdma(HS.at[erows(b), :H], CS.at[erows(b), :H], 24 + b)
-
-    def grad_copy(b):
-        return rdma(R2.at[erows(b), :H], R2.at[erows(b), H:], 34 + b)
+    lat_copy = rdma(HS.at[:, :H], CS.at[:, :H], 6)
+    grad_copy = rdma(R2.at[:NE * NS, :H], R2.at[:NE * NS, H:], 7)
+
+    def stage_rows(dst, src):
+        def one(b, carry):
+            dst[erows(b), :H] = rows_of(src[edges(b)])
+            return carry
+        lax.fori_loop(0, NB, one, 0)
 
     loads[2].wait()
-    for j in (5, 6, 4):
-        w_send(0, j)
-    loads[3].wait()
-    loads[4].wait()
-
-    def lat_send(b, carry):
-        HS[erows(b), :H] = rows_of(E1[0, edges(b)])
-        lat_copy(b).start()
-        return carry
-
-    lat_send(0, 0)
-    w_send(0, J_EW2)
-    lax.fori_loop(1, NB, lat_send, 0)
-    loads[6].wait()
-    loads[7].wait()
-    for j in (1, 2, 0):
-        w_send(0, j)
-    for j in (5, 6, 4, 3, 1, 2, 0):
-        w_send(1, j)
-
-    loads[8].wait()
-
-    def grad_send(b, carry):
-        R2[erows(b), :H] = rows_of(E1[1, edges(b)])
-        grad_copy(b).start()
-        return carry
-
-    lax.fori_loop(0, NB, grad_send, 0)
-    loads[10].wait()
-    loads[11].wait()
+    for k in range(2):
+        w_packs(k)
+        w_copies[k].start()
+    wait_all(loads[3:5])
+    stage_rows(HS, E1.at[0])
+    lat_copy.start()
+    w_packs(2)
+    w_copies[2].start()
+    wait_all(loads[5:])
+    w_packs(3)
+    w_packs(4)
+    stage_rows(R2, E1.at[1])
     NF[2] = NST[3].astype(F32)
     node_g = rdma(NF.at[2], NF.at[3], 3)
-    node_g.start()
-
-    def select(dst, base):
-        def one(b, carry):
-            rows = lax.broadcasted_iota(jnp.int32, (ROWS, BR), 0)
-            dst[b] = jnp.where(rows == flat[base + b], 1.0, 0.0).astype(BF)
+
+    column = lax.broadcasted_iota(jnp.int32, (NS, ROWS), 1) - lax.broadcasted_iota(jnp.int32, (NS, ROWS), 0)
+
+    def select(dst, ids):
+        def one(i, carry):
+            two = [jnp.where(column == ids[2 * i + k] * NS, 1.0, 0.0) for k in range(2)]
+            at = pl.ds(pl.multiple_of(i * 2 * NS, 2 * NS), 2 * NS)
+            dst[at] = jnp.concatenate(two, axis=0).astype(BF)
             return carry
-        lax.fori_loop(0, NB, one, 0)
-
-    select(KR, NB)
-    select(KS, 0)
+        lax.fori_loop(0, NE // 2, one, 0, unroll=5)
+
+    select(KR, rcv)
 
     def node_in(dst, staged, received):
         own, got = rows_of(NST[staged]), rows_of(NF[received])
@@ -226,21 +224,19 @@
         return dot_cols(dout[:, :H], ref[layer, 0]) + dot_cols(dout[:, H:], ref[layer, 1])
 
     def layer_fwd(layer, src, dst):
-        if layer == 0:
-            w_recv(0, 5)
-            w_recv(0, 6)
+        w_recv(0 if layer == 0 else 4)
         PS[...] = (dot(VF[layer], full1(W1E, layer, 1)) + b1e[layer:layer + 1]).reshape(NN, NS, D)
         PR[...] = dot(VF[layer], full1(W1E, layer, 2)).reshape(NN, NS, D)
         if layer == 0:
-            w_recv(0, 4)
-            w_recv(0, 3)
-            loads[5].wait()
+            w_recv(1)
+            w_recv(2)
+            lat_copy.wait()
+            start_all(w_copies[3:])
         c0, gam, bet = (vec_row(layer, r, False) for r in range(3))
         AG[...] = jnp.zeros_like(AG)
 
         def edge(b, carry):
             if layer == 0:
-                lat_copy(b).wait()
                 src[ot, edges(b)] = CS[erows(b), :H].reshape(BE, NS, H).astype(BF)
             for i in range(BE):
                 GA[i * NS:(i + 1) * NS] = PS[snd[b * BE + i]] + PR[rcv[b * BE + i]]
@@ -253,7 +249,7 @@
             CS[erows(b)] = cen
             normed, unused = norm_parts(cen)
             msg = (normed * gam + bet).astype(BF)
-            AG[...] += dot(KR[b], msg)
+            AG[...] += dot_rows(KR[erows(b)], msg)
             new = lat + msg.astype(F32)
             dst[0, edges(b)] = new[:, :H].reshape(BE, NS, H).astype(BF)
             dst[1, edges(b)] = new[:, H:].reshape(BE, NS, H).astype(BF)
@@ -261,10 +257,9 @@
 
         lax.fori_loop(0, NB, edge, 0)
         if layer == 0:
-            for cp in spills:
-                cp.start()
-            for j in (1, 2, 0):
-                w_recv(0, j)
+            start_all(spills)
+            start_all([grad_copy, node_g])
+            w_recv(3)
         SF[layer] = AG[...].astype(BF)
         lat = VF[layer]
         hidden = dot(lat, full1(W1N, layer, 0)) + dot(SF[layer], full1(W1N, layer, 1)) + b1n[layer:layer + 1]
@@ -281,35 +276,32 @@
     fills = [pltpu.make_async_copy(spill.at[0], HS, spsem.at[2]), pltpu.make_async_copy(spill.at[1], CS, spsem.at[3])]
 
     layer_fwd(0, E0, E1)
-    for j in range(7):
-        w_recv(1, j)
-    loads[9].wait()
-
-    def grad_recv(b, carry):
-        grad_copy(b).wait()
+    select(KS, snd)
+    wait_all(spills)
+    layer_fwd(1, E1, E2)
+    grad_copy.wait()
+
+    def grad_rows(b, carry):
         DE[ot, edges(b)] = R2[erows(b), H:].reshape(BE, NS, H).astype(BF)
         return carry
 
-    lax.fori_loop(0, NB, grad_recv, 0)
+    lax.fori_loop(0, NB, grad_rows, 0)
     for peer in peers:
         pl.semaphore_signal(csem.at[0], inc=1, device_id=peer, device_id_type=MESH)
     node_g.wait()
     node_in(DN, 2, 3)
-    for cp in spills:
-        cp.wait()
-    layer_fwd(1, E1, E2)
 
     def chunk(c):
         return 1 - c // 7, c % 7
 
-    def g_copy(c, k, src, dst, peer):
+    def g_copy(c, send, k, src, dst, peer):
         return pltpu.make_async_remote_copy(
-            src_ref=src, dst_ref=dst, send_sem=gssem.at[c, k], recv_sem=grsem.at[c, k],
+            src_ref=src, dst_ref=dst, send_sem=gssem.at[c % 7, send], recv_sem=grsem.at[c % 7, k],
             device_id=peer, device_id_type=MESH)
 
     def core_copy(c):
         layer, j = chunk(c)
-        return g_copy(c, 0, G.at[layer, ot, j], R2.at[j * H:(j + 1) * H], partner)
+        return g_copy(c, 0, 0, G.at[layer, ot, j], R2.at[j * H:(j + 1) * H], partner)
 
     def landing(c):
         layer, j = chunk(c)
@@ -326,21 +318,21 @@
 
     def a_copies(c):
         land = landing(c)
-        return [g_copy(c, 1, strip(c, 64 - half_p, 64), land(0, 64), x_peer),
-                g_copy(c, 2, strip(c, 320 - half_q, 64), land(64, 64), y_peer)]
+        return [g_copy(c, 1, 1, strip(c, 64 - half_p, 64), land(0, 64), x_peer),
+                g_copy(c, 2, 2, strip(c, 320 - half_q, 64), land(64, 64), y_peer)]
 
     def b_copies(c):
         land = landing(c)
-        return [g_copy(c, 3, strip(c, half_p + 32 - cy * 32, 32), land(128, 32), y_peer),
-                g_copy(c, 4, strip(c, half_q + 32 - cx * 32, 32), land(160, 32), x_peer)]
+        return [g_copy(c, 1, 3, strip(c, half_p + 32 - cy * 32, 32), land(128, 32), y_peer),
+                g_copy(c, 2, 4, strip(c, half_q + 32 - cx * 32, 32), land(160, 32), x_peer)]
 
     def c_copies(c):
         ref_p, ref_q = strip(c, quarter_p, 32, True), strip(c, quarter_q, 32, True)
-        return [g_copy(c, 5, ref_p, ref_p, y_peer), g_copy(c, 6, ref_q, ref_q, x_peer)]
+        return [g_copy(c, 1, 5, ref_p, ref_p, y_peer), g_copy(c, 2, 6, ref_q, ref_q, x_peer)]
 
     def d_copies(c):
         ref_p, ref_q = strip(c, half_p, 64, True), strip(c, half_q, 64, True)
-        return [g_copy(c, 7, ref_p, ref_p, x_peer), g_copy(c, 8, ref_q, ref_q, y_peer)]
+        return [g_copy(c, 1, 7, ref_p, ref_p, x_peer), g_copy(c, 2, 8, ref_q, ref_q, y_peer)]
 
     def store_copies(c):
         layer, j = chunk(c)
@@ -352,15 +344,7 @@
             pairs = [(src, o_nw1.at[layer, j - J_NW1])]
         else:
             pairs = [(src, o_ew1.at[layer, j - J_EW1])]
-        return [pltpu.make_async_copy(a, b, osem.at[c, k]) for k, (a, b) in enumerate(pairs)]
-
-    def wait_all(copies):
-        for cp in copies:
-            cp.wait()
-
-    def start_all(copies):
-        for cp in copies:
-            cp.start()
+        return [pltpu.make_async_copy(a, b, osem.at[c % 7, k]) for k, (a, b) in enumerate(pairs)]
 
     def stage0(c):
         core_copy(c).start()
@@ -392,6 +376,8 @@
 
     def stage5(c):
         wait_all(d_copies(c))
+        if c >= 7:
+            wait_all(store_copies(c - 7))
         start_all(store_copies(c))
 
     def run(stage, chunks):
@@ -413,7 +399,7 @@
             G[layer, half, j, :, :H] = value[:H]
             G[layer, half, j, :, H:] = value[H:]
 
-    def put_w1(layer, j, value, add):
+    def put_w1(layer, j, value, add=False):
         for half in range(2):
             if add:
                 G[layer, half, j] += value[half * H:(half + 1) * H]
@@ -448,9 +434,9 @@
         nodes, edge_w2, edge_w1 = (node1, edge1[:1], edge1[1:]) if layer else (node0, edge0[:1], edge0[1:])
         pl.semaphore_wait(csem.at[1 - layer], 3 if layer == 1 else 1)
         stage0(nodes[0])
-        put_w1(layer, J_NW1, dot_rows(VF[layer], d_hid), False)
+        put_w1(layer, J_NW1, dot_rows(VF[layer], d_hid))
         stage0(nodes[1])
-        put_w1(layer, J_NW1 + 1, dot_rows(SF[layer], d_hid), False)
+        put_w1(layer, J_NW1 + 1, dot_rows(SF[layer], d_hid))
         stage0(nodes[2])
         DV[...] = d_node + dot_cols(d_hid, full1(W1N, layer, 0))
         PS[...] = dot_cols(d_hid, full1(W1N, layer, 1)).reshape(NN, NS, D)
@@ -473,8 +459,8 @@
             new = d_edge + dot_cols(d_hid, full1(W1E, layer, 0))
             DE[0, edges(b)] = new[:, :H].reshape(BE, NS, H).astype(BF)
             DE[1, edges(b)] = new[:, H:].reshape(BE, NS, H).astype(BF)
-            AG[...] += dot(KS[b], d_hid)
-            PR[...] += dot(KR[b], d_hid).reshape(NN, NS, D)
+            AG[...] += dot_rows(KS[erows(b)], d_hid)
+            PR[...] += dot_rows(KR[erows(b)], d_hid).reshape(NN, NS, D)
             for stage, chunks, first in plan[layer]:
                 for i, c in enumerate(chunks):
                     pl.when(b == first + i)(functools.partial(stage, c))
@@ -486,9 +472,9 @@
                 cp.start()
         run(stage0, edge_w2 + edge_w1[:1])
         d_ps, d_pr = AG[...].astype(BF), rows_of(PR[...]).astype(BF)
-        put_w1(layer, J_EW1 + 1, dot_rows(VF[layer], d_ps), False)
+        put_w1(layer, J_EW1 + 1, dot_rows(VF[layer], d_ps))
         stage0(edge_w1[1])
-        put_w1(layer, J_EW1 + 2, dot_rows(VF[layer], d_pr), False)
+        put_w1(layer, J_EW1 + 2, dot_rows(VF[layer], d_pr))
         stage0(edge_w1[2])
         DN[...] = (DV[...] + dot_cols(d_ps, full1(W1E, layer, 1))
                    + dot_cols(d_pr, full1(W1E, layer, 2))).astype(BF)
@@ -515,17 +501,14 @@
 
     lax.fori_loop(0, NB, out_stage, 0)
     pl.semaphore_wait(csem.at[2], 1)
-    small0 = rdma(SM.at[0], SM.at[1], 6)
+    small0 = rdma(SM.at[0], SM.at[1], 2)
     small0.start()
     node_o = [rdma(NF.at[0], NF.at[1], 4), rdma(NF.at[2], NF.at[3], 5)]
     for cp in node_o:
         cp.start()
 
-    def out_copy(b):
-        return rdma(HS.at[erows(b)], CS.at[erows(b)], 44 + b)
-
-    for b in range(NB):
-        out_copy(b).start()
+    out_copy = rdma(HS, CS, 6)
+    out_copy.start()
     stores = [
         (E2.at[tp], o_e.at[:, mine]), (DE.at[tp], o_de.at[:, mine]),
         (NST.at[0], o_n.at[:, mine]), (NST.at[2], o_dn.at[:, mine]),
@@ -539,12 +522,12 @@
         NST[2 * k + 1] = NF[2 * k + 1].astype(BF)
 
     def out_recv(b, carry):
-        out_copy(b).wait()
         E1[0, edges(b)] = CS[erows(b), :H].reshape(BE, NS, H).astype(BF)
         E1[1, edges(b)] = CS[erows(b), H:].reshape(BE, NS, H).astype(BF)
         return carry
 
     run(stage3, node0)
+    out_copy.wait()
     lax.fori_loop(0, NB, out_recv, 0)
     more = [
         (E1.at[0], o_e.at[:, theirs]), (E1.at[1], o_de.at[:, theirs]),
@@ -555,17 +538,13 @@
         cp.start()
     small0.wait()
     SM[2] = SM[0] + SM[1]
-    small1 = pltpu.make_async_remote_copy(
-        src_ref=SM.at[2], dst_ref=SM.at[3], send_sem=ssem.at[7], recv_sem=rsem.at[7],
-        device_id=x_peer, device_id_type=MESH)
+    small1 = rdma(SM.at[2], SM.at[3], 3, x_peer)
     small1.start()
     run(stage2, edge0)
     run(stage4, node0)
     small1.wait()
     SM[4] = SM[2] + SM[3]
-    small2 = pltpu.make_async_remote_copy(
-        src_ref=SM.at[4], dst_ref=SM.at[5], send_sem=ssem.at[54], recv_sem=rsem.at[54],
-        device_id=y_peer, device_id_type=MESH)
+    small2 = rdma(SM.at[4], SM.at[5], 13, y_peer)
     small2.start()
     run(stage3, edge0)
     small2.wait()
@@ -579,7 +558,7 @@
                 ref_v[k, layer:layer + 1] = jnp.where(tp == 0, one[:, :H], one[:, H:])
     run(stage4, edge0)
     run(stage5, node0 + edge0)
-    for c in node1 + edge1 + node0 + edge0:
+    for c in node0 + edge0:
         wait_all(store_copies(c))
     for cp in stores + more:
         cp.wait()
@@ -599,24 +578,52 @@
     node = (ROWS, D)
     scratch = [
         v((2, 3, 2, H, D), BF), v((2, 2, D, H), BF), v((2, 2, 2, H, D), BF), v((2, 2, D, H), BF),
-        *[v((2, 3, 2, H), F32)] * 2, *[v((NB, ROWS, BR), BF)] * 2, *[v((2, NE, NS, H), BF)] * 4,
+        *[v((2, 3, 2, H), F32)] * 2, *[v((NE * NS, ROWS), BF)] * 2, *[v((2, NE, NS, H), BF)] * 4,
         v((NE * NS, D), F32), v((NE * NS, D), F32), v((7 * (H + 192), D), F32), v((2, 2, 7, H, D), F32),
         v((NN, NS, D), F32), v((NN, NS, D), F32), v((BR, D), F32), v(node, F32),
         v((4, NN, NS, H), BF), v((4, NN, NS, H), F32),
         v((3, *node), BF), v((2, *node), BF), v((2, *node), F32), v((2, *node), F32),
         v(node, BF), v(node, F32), v((6, 16, D), F32),
-        dma((12,)), dma((56,)), dma((56,)), pltpu.SemaphoreType.REGULAR((3,)), dma((4,)),
-        dma((14, 9)), dma((14, 9)), dma((14, 2)),
+        dma((12,)), dma((14,)), dma((14,)), pltpu.SemaphoreType.REGULAR((3,)), dma((4,)),
+        dma((7, 3)), dma((7, 9)), dma((7, 2)),
     ]
     return pl.pallas_call(
         body,
         out_shape=[jax.ShapeDtypeStruct(*o) for o in outs],
-        in_specs=[any_spec] * 8 + [vm] * 5 + [sm] * 2,
+        in_specs=[any_spec] * 8 + [vm] * 4 + [sm] * 2,
         out_specs=[any_spec] * 8 + [vm] * 4 + [any_spec],
         scratch_shapes=scratch,
         compiler_params=pltpu.CompilerParams(
             collective_id=0, has_side_effects=True, vmem_limit_bytes=67043328),
     )(*args)
+
+
+def mover(*refs):
+    n = (len(refs) - 2) // 3
+    pieces = []
+    for src, dst, buf in zip(refs[:n], refs[n:2 * n], refs[2 * n:]):
+        step = -(-src.shape[0] // (4 if src.size > 1 << 18 else 1))
+        for lo in range(0, src.shape[0], step):
+            at = pl.ds(lo, min(step, src.shape[0] - lo))
+            k = len(pieces)
+            pieces.append((pltpu.make_async_copy(src.at[at], buf.at[at], refs[-2].at[k]),
+                           pltpu.make_async_copy(buf.at[at], dst.at[at], refs[-1].at[k])))
+    for get, unused in pieces:
+        get.start()
+    for get, put in pieces:
+        get.wait()
+        put.start()
+    for unused, put in pieces:
+        put.wait()
+
+
+def move(arrays):
+    any_spec = pl.BlockSpec(memory_space=pl.ANY)
+    shapes = [jax.ShapeDtypeStruct(x.shape, x.dtype) for x in arrays]
+    return pl.pallas_call(
+        mover, out_shape=shapes, in_specs=[any_spec] * len(arrays), out_specs=[any_spec] * len(arrays),
+        scratch_shapes=[pltpu.VMEM(x.shape, x.dtype) for x in arrays] + [pltpu.SemaphoreType.DMA((24,))] * 2,
+        compiler_params=pltpu.CompilerParams(vmem_limit_bytes=67043328))(*arrays)
 
 
 def solution(mesh):
@@ -631,12 +638,11 @@
         def swap(x):
             return jnp.transpose(x, (1, 0, 2))
 
-        ids = jnp.stack([senders, receivers])
-        flat = ids[:, :, None] * NS + jnp.arange(NS, dtype=jnp.int32)
         outs = compute(
             swap(node_lat), swap(edge_lat), swap(grad_node), swap(grad_edge), edge_w1, edge_w2, node_w1, node_w2,
-            edge_b1, node_b1, swap(edge_vec), swap(node_vec), flat.reshape(2 * NB, 1, BR), senders, receivers)
-        o_ew1, o_ew2, o_nw1, o_nw2, o_be, o_bn, o_ve, o_vn = outs[4:12]
+            edge_b1, node_b1, swap(edge_vec), swap(node_vec), senders, receivers)
+        outs = move(outs[:12])
+        o_ew1, o_ew2, o_nw1, o_nw2, o_be, o_bn, o_ve, o_vn = outs[4:]
         return tuple(swap(x) for x in outs[:4]) + (o_ew1, o_be, o_ew2, swap(o_ve), o_nw1, o_bn, o_nw2, swap(o_vn))
 
     return jax.shard_map(local_step, mesh=mesh, in_specs=in_specs, out_specs=out_specs, check_vma=False)

time: 187 us -> 179 us (0.957)
  local copies, waits for them, and re-layouts: 18.2 us -> 0 us
  Pallas kernels: 167 us -> 178 us
    unnamed x32 -> x0, local copies, waits for them, and re-layouts: 16 us -> none
    pallas_call x0 -> x1, Pallas kernels: none -> 9.86 us  [move(): pl.pallas_call(mover, out_shape=shapes, in_specs=[any_spec] * len(arrays)...]
where the time goes in v4:
time: 179 us; the launch traced here: 178 us
  Pallas kernels  178 us (99%)
    pallas_call x1, Pallas kernels, compute(): pl.pallas_call(body, out_shape=[jax.ShapeDtypeStruct(*o) for o in outs],...  168 us
    pallas_call x1, Pallas kernels, move(): pl.pallas_call(mover, out_shape=shapes, in_specs=[any_spec] * len(arrays)...  9.86 us

profile of v4, /device:TPU:0, one launch (start us, length us, event | category | flops | bytes accessed | tf_op | source)
XLA Modules:
  0.0 178.4 jit_solution(5238448928986056066)
XLA Ops:
  0.6 167.7 %shard_map.229 = (bf16[42,16,256]{2,1,0:T(8,128)(2,1)}, bf16[300,16,256]{2,1,0:T(8,128)(2,1)}, bf16[42,16,256]{2,1,0:T(8,128)(2,1)}, bf16[300,16,256]{2,1,0:T(8,...) custom-call(bf16[42,16,256]{2,1,0:T(8,128)(2,1)} %bitcast.14, ...), custom_call_target="tpu_custom_call" | custom-call | tf_op jit(solution)/shard_map/pallas_call | solution.py:590
  168.4 9.9 %shard_map.230 = (bf16[42,16,256]{2,1,0:T(8,128)(2,1)}, bf16[300,16,256]{2,1,0:T(8,128)(2,1)}, bf16[42,16,256]{2,1,0:T(8,128)(2,1)}, bf16[300,16,256]{2,1,0:T(8,...) custom-call(bf16[42,16,256]{2,1,0:T(8,128)(2,1)} %get-tuple-element., ...), custom_call_target="tpu_custom_call" | custom-call | tf_op jit(solution)/shard_map/pallas_call | solution.py:623

commit v5 on v4

--- a/solution.py
+++ b/solution.py
@@ -19,7 +19,7 @@
 ROWS = NN * NS
 NB = 10
 BE = NE // NB
-BR = BE * NS
+WIDE = 60
 
 
 def dot(lhs, rhs, lc=1, rc=0):
@@ -153,11 +153,11 @@
         for j in range(lo, lo + n):
             w_unpack(layer, j, G[0, layer, j])
 
-    def edges(b):
-        return pl.ds(b * BE, BE)
-
-    def erows(b):
-        return pl.ds(pl.multiple_of(b * BR, BR), BR)
+    def edges(b, n=BE):
+        return pl.ds(b * n, n)
+
+    def erows(b, n=BE):
+        return pl.ds(pl.multiple_of(b * n * NS, n * NS), n * NS)
 
     lat_copy = rdma(HS.at[:, :H], CS.at[:, :H], 6)
     grad_copy = rdma(R2.at[:NE * NS, :H], R2.at[:NE * NS, H:], 7)
@@ -237,25 +237,25 @@
 
         def edge(b, carry):
             if layer == 0:
-                src[ot, edges(b)] = CS[erows(b), :H].reshape(BE, NS, H).astype(BF)
-            for i in range(BE):
-                GA[i * NS:(i + 1) * NS] = PS[snd[b * BE + i]] + PR[rcv[b * BE + i]]
-            lat = cat(rows_of(src[0, edges(b)]), rows_of(src[1, edges(b)]))
+                src[ot, edges(b, WIDE)] = CS[erows(b, WIDE), :H].reshape(WIDE, NS, H).astype(BF)
+            for i in range(WIDE):
+                GA[i * NS:(i + 1) * NS] = PS[snd[b * WIDE + i]] + PR[rcv[b * WIDE + i]]
+            lat = cat(rows_of(src[0, edges(b, WIDE)]), rows_of(src[1, edges(b, WIDE)]))
             hidden = dot(lat.astype(BF), full1(W1E, layer, 0)) + GA[...]
-            HS[erows(b)] = hidden
+            HS[erows(b, WIDE)] = hidden
             act = (hidden * gate(hidden)).astype(BF)
             out = second(act, W2E, layer) + c0
             cen = out - mean_cols(out)
-            CS[erows(b)] = cen
+            CS[erows(b, WIDE)] = cen
             normed, unused = norm_parts(cen)
             msg = (normed * gam + bet).astype(BF)
-            AG[...] += dot_rows(KR[erows(b)], msg)
+            AG[...] += dot_rows(KR[erows(b, WIDE)], msg)
             new = lat + msg.astype(F32)
-            dst[0, edges(b)] = new[:, :H].reshape(BE, NS, H).astype(BF)
-            dst[1, edges(b)] = new[:, H:].reshape(BE, NS, H).astype(BF)
+            dst[0, edges(b, WIDE)] = new[:, :H].reshape(WIDE, NS, H).astype(BF)
+            dst[1, edges(b, WIDE)] = new[:, H:].reshape(WIDE, NS, H).astype(BF)
             return carry
 
-        lax.fori_loop(0, NB, edge, 0)
+        lax.fori_loop(0, NE // WIDE, edge, 0)
         if layer == 0:
             start_all(spills)
             start_all([grad_copy, node_g])
@@ -453,7 +453,7 @@
             for i in range(BE):
                 GA[i * NS:(i + 1) * NS] = PS[rcv[b * BE + i]]
             d_edge = cat(rows_of(DE[0, edges(b)]), rows_of(DE[1, edges(b)]))
-            d_hid = mlp_bwd(d_edge + GA[...], CS[erows(b)], HS[erows(b)], gam, W2E, layer, layer * 8 + 4, J_EW2, True)
+            d_hid = mlp_bwd(d_edge + GA[:BE * NS], CS[erows(b)], HS[erows(b)], gam, W2E, layer, layer * 8 + 4, J_EW2, True)
             lat = cat(rows_of(src[0, edges(b)]), rows_of(src[1, edges(b)])).astype(BF)
             put_w1(layer, J_EW1, dot_rows(lat, d_hid), True)
             new = d_edge + dot_cols(d_hid, full1(W1E, layer, 0))
@@ -580,7 +580,7 @@
         v((2, 3, 2, H, D), BF), v((2, 2, D, H), BF), v((2, 2, 2, H, D), BF), v((2, 2, D, H), BF),
         *[v((2, 3, 2, H), F32)] * 2, *[v((NE * NS, ROWS), BF)] * 2, *[v((2, NE, NS, H), BF)] * 4,
         v((NE * NS, D), F32), v((NE * NS, D), F32), v((7 * (H + 192), D), F32), v((2, 2, 7, H, D), F32),
-        v((NN, NS, D), F32), v((NN, NS, D), F32), v((BR, D), F32), v(node, F32),
+        v((NN, NS, D), F32), v((NN, NS, D), F32), v((WIDE * NS, D), F32), v(node, F32),
         v((4, NN, NS, H), BF), v((4, NN, NS, H), F32),
         v((3, *node), BF), v((2, *node), BF), v((2, *node), F32), v((2, *node), F32),
         v(node, BF), v(node, F32), v((6, 16, D), F32),

time: 179 us -> 173 us (0.966)
  Pallas kernels: 178 us -> 172 us
    pallas_call x1, Pallas kernels: 168 us -> 162 us  [compute(): pl.pallas_call(body, out_shape=[jax.ShapeDtypeStruct(*o) for o in outs],...]
where the time goes in v5:
time: 173 us
  Pallas kernels  172 us (99%)
    pallas_call x1, Pallas kernels, compute(): pl.pallas_call(body, out_shape=[jax.ShapeDtypeStruct(*o) for o in outs],...  162 us
    pallas_call x1, Pallas kernels, move(): pl.pallas_call(mover, out_shape=shapes, in_specs=[any_spec] * len(arrays)...  9.86 us

profile of v5, /device:TPU:0, one launch (start us, length us, event | category | flops | bytes accessed | tf_op | source)
XLA Modules:
  0.0 172.8 jit_solution(8463860779115201029)
XLA Ops:
  0.6 162.2 %shard_map.229 = (bf16[42,16,256]{2,1,0:T(8,128)(2,1)}, bf16[300,16,256]{2,1,0:T(8,128)(2,1)}, bf16[42,16,256]{2,1,0:T(8,128)(2,1)}, bf16[300,16,256]{2,1,0:T(8,...) custom-call(bf16[42,16,256]{2,1,0:T(8,128)(2,1)} %bitcast.14, ...), custom_call_target="tpu_custom_call" | custom-call | tf_op jit(solution)/shard_map/pallas_call | solution.py:590
  162.8 9.9 %shard_map.230 = (bf16[42,16,256]{2,1,0:T(8,128)(2,1)}, bf16[300,16,256]{2,1,0:T(8,128)(2,1)}, bf16[42,16,256]{2,1,0:T(8,128)(2,1)}, bf16[300,16,256]{2,1,0:T(8,...) custom-call(bf16[42,16,256]{2,1,0:T(8,128)(2,1)} %get-tuple-element., ...), custom_call_target="tpu_custom_call" | custom-call | tf_op jit(solution)/shard_map/pallas_call | solution.py:623

commit v6 on v5

--- a/solution.py
+++ b/solution.py
@@ -15,6 +15,7 @@
 NN = 42
 NE = 300
 D = 512
+PAIR = 2 * NS
 H = 256
 ROWS = NN * NS
 NB = 10
@@ -27,11 +28,11 @@
 
 
 def dot_rows(lhs, rhs):
-    return dot(lhs, rhs, 0, 0)
+    return dot(lhs, rhs, 0)
 
 
 def dot_cols(lhs, rhs):
-    return dot(lhs, rhs, 1, 1)
+    return dot(lhs, rhs, rc=1)
 
 
 def cat(lhs, rhs):
@@ -159,7 +160,10 @@
     def erows(b, n=BE):
         return pl.ds(pl.multiple_of(b * n * NS, n * NS), n * NS)
 
-    lat_copy = rdma(HS.at[:, :H], CS.at[:, :H], 6)
+    def lat_copy(b):
+        at = erows(b, WIDE)
+        return rdma(HS.at[at, :H], CS.at[at, :H], 14 + b)
+
     grad_copy = rdma(R2.at[:NE * NS, :H], R2.at[:NE * NS, H:], 7)
 
     def stage_rows(dst, src):
@@ -174,9 +178,10 @@
         w_copies[k].start()
     wait_all(loads[3:5])
     stage_rows(HS, E1.at[0])
-    lat_copy.start()
+    lat_copy(0).start()
     w_packs(2)
     w_copies[2].start()
+    lat_copy(1).start()
     wait_all(loads[5:])
     w_packs(3)
     w_packs(4)
@@ -189,7 +194,7 @@
     def select(dst, ids):
         def one(i, carry):
             two = [jnp.where(column == ids[2 * i + k] * NS, 1.0, 0.0) for k in range(2)]
-            at = pl.ds(pl.multiple_of(i * 2 * NS, 2 * NS), 2 * NS)
+            at = pl.ds(pl.multiple_of(i * PAIR, PAIR), PAIR)
             dst[at] = jnp.concatenate(two, axis=0).astype(BF)
             return carry
         lax.fori_loop(0, NE // 2, one, 0, unroll=5)
@@ -207,7 +212,7 @@
     node_x.wait()
     node_in(VF.at[0], 0, 1)
 
-    def vec_row(layer, row, node):
+    def vec_row(layer, row, node=False):
         ref = VN if node else VE
         return cat(ref[0, row, layer:layer + 1], ref[1, row, layer:layer + 1])
 
@@ -223,20 +228,30 @@
     def second_t(dout, ref, layer):
         return dot_cols(dout[:, :H], ref[layer, 0]) + dot_cols(dout[:, H:], ref[layer, 1])
 
+    def add_message(dst, b, n, lat, msg):
+        new = lat + msg.astype(F32)
+        dst[0, edges(b, n)] = new[:, :H].reshape(n, NS, H).astype(BF)
+        dst[1, edges(b, n)] = new[:, H:].reshape(n, NS, H).astype(BF)
+
     def layer_fwd(layer, src, dst):
-        w_recv(0 if layer == 0 else 4)
+        w_recv(4 * layer)
         PS[...] = (dot(VF[layer], full1(W1E, layer, 1)) + b1e[layer:layer + 1]).reshape(NN, NS, D)
         PR[...] = dot(VF[layer], full1(W1E, layer, 2)).reshape(NN, NS, D)
-        if layer == 0:
+        if layer:
+            start_all([grad_copy, node_g])
+        else:
             w_recv(1)
             w_recv(2)
-            lat_copy.wait()
-            start_all(w_copies[3:])
-        c0, gam, bet = (vec_row(layer, r, False) for r in range(3))
+            lat_copy(2).start()
+        c0, gam, bet = (vec_row(layer, r) for r in range(3))
         AG[...] = jnp.zeros_like(AG)
 
         def edge(b, carry):
-            if layer == 0:
+            if not layer:
+                lat_copy(b).wait()
+                pl.when(b < 2)(lambda: lat_copy(b + 3).start())
+                pl.when(b == 2)(w_copies[3].start)
+                pl.when(b == 3)(w_copies[4].start)
                 src[ot, edges(b, WIDE)] = CS[erows(b, WIDE), :H].reshape(WIDE, NS, H).astype(BF)
             for i in range(WIDE):
                 GA[i * NS:(i + 1) * NS] = PS[snd[b * WIDE + i]] + PR[rcv[b * WIDE + i]]
@@ -250,15 +265,13 @@
             normed, unused = norm_parts(cen)
             msg = (normed * gam + bet).astype(BF)
             AG[...] += dot_rows(KR[erows(b, WIDE)], msg)
-            new = lat + msg.astype(F32)
-            dst[0, edges(b, WIDE)] = new[:, :H].reshape(WIDE, NS, H).astype(BF)
-            dst[1, edges(b, WIDE)] = new[:, H:].reshape(WIDE, NS, H).astype(BF)
+            if not layer:
+                add_message(dst, b, WIDE, lat, msg)
             return carry
 
         lax.fori_loop(0, NE // WIDE, edge, 0)
-        if layer == 0:
+        if not layer:
             start_all(spills)
-            start_all([grad_copy, node_g])
             w_recv(3)
         SF[layer] = AG[...].astype(BF)
         lat = VF[layer]
@@ -278,7 +291,7 @@
     layer_fwd(0, E0, E1)
     select(KS, snd)
     wait_all(spills)
-    layer_fwd(1, E1, E2)
+    layer_fwd(1, E1, None)
     grad_copy.wait()
 
     def grad_rows(b, carry):
@@ -305,7 +318,7 @@
 
     def landing(c):
         layer, j = chunk(c)
-        if layer == 1:
+        if layer:
             return lambda lo, n: R2.at[7 * H + j * 192 + lo:7 * H + j * 192 + lo + n]
         return lambda lo, n: G.at[1, tp, j, lo:lo + n]
 
@@ -387,8 +400,8 @@
     node1, edge1, node0, edge0 = (list(range(*ends)) for ends in ((0, 3), (3, 7), (7, 10), (10, 14)))
 
     plan = {
-        1: [(stage1, node1, 0), (stage2, node1, 4), (stage3, node1, 7)],
-        0: [(stage5, node1, 0), (stage2, edge1, 1), (stage1, node0, 5), (stage3, edge1, 5), (stage4, edge1[:2], 8)],
+        1: [(stage2, node1, 3), (stage3, node1, 7)],
+        0: [(stage2, edge1, 0), (stage5, node1, 3), (stage3, edge1, 5), (stage4, edge1[:2], 8)],
     }
 
     def put_w2(layer, j, half, value, add):
@@ -436,16 +449,19 @@
         stage0(nodes[0])
         put_w1(layer, J_NW1, dot_rows(VF[layer], d_hid))
         stage0(nodes[1])
+        stage1(nodes[0])
         put_w1(layer, J_NW1 + 1, dot_rows(SF[layer], d_hid))
         stage0(nodes[2])
+        stage1(nodes[1])
         DV[...] = d_node + dot_cols(d_hid, full1(W1N, layer, 0))
         PS[...] = dot_cols(d_hid, full1(W1N, layer, 1)).reshape(NN, NS, D)
+        stage1(nodes[2])
         for j in (J_EW2, J_EW1):
             G[layer, :, j] = jnp.zeros((2, H, D), F32)
         AG[...] = jnp.zeros_like(AG)
         PR[...] = jnp.zeros_like(PR)
-        gam = vec_row(layer, 1, False)
-        if layer == 0:
+        gam, bet = vec_row(layer, 1), vec_row(layer, 2)
+        if not layer:
             for cp in fills:
                 cp.wait()
 
@@ -454,8 +470,11 @@
                 GA[i * NS:(i + 1) * NS] = PS[rcv[b * BE + i]]
             d_edge = cat(rows_of(DE[0, edges(b)]), rows_of(DE[1, edges(b)]))
             d_hid = mlp_bwd(d_edge + GA[:BE * NS], CS[erows(b)], HS[erows(b)], gam, W2E, layer, layer * 8 + 4, J_EW2, True)
-            lat = cat(rows_of(src[0, edges(b)]), rows_of(src[1, edges(b)])).astype(BF)
-            put_w1(layer, J_EW1, dot_rows(lat, d_hid), True)
+            lat = cat(rows_of(src[0, edges(b)]), rows_of(src[1, edges(b)]))
+            put_w1(layer, J_EW1, dot_rows(lat.astype(BF), d_hid), True)
+            if layer:
+                normed, unused = norm_parts(CS[erows(b)])
+                add_message(E2, b, BE, lat, (normed * gam + bet).astype(BF))
             new = d_edge + dot_cols(d_hid, full1(W1E, layer, 0))
             DE[0, edges(b)] = new[:, :H].reshape(BE, NS, H).astype(BF)
             DE[1, edges(b)] = new[:, H:].reshape(BE, NS, H).astype(BF)
@@ -467,10 +486,11 @@
             return carry
 
         lax.fori_loop(0, NB, edge, 0)
-        if layer == 1:
+        if layer:
             for cp in fills:
                 cp.start()
         run(stage0, edge_w2 + edge_w1[:1])
+        run(stage4, node1[:2] if layer else edge1[2:])
         d_ps, d_pr = AG[...].astype(BF), rows_of(PR[...]).astype(BF)
         put_w1(layer, J_EW1 + 1, dot_rows(VF[layer], d_ps))
         stage0(edge_w1[1])
@@ -481,10 +501,9 @@
 
     layer_bwd(1, E1)
     run(stage1, edge1)
-    run(stage4, node1)
+    run(stage4, node1[2:])
     pl.semaphore_signal(csem.at[1], inc=1, device_id=partner, device_id_type=MESH)
     layer_bwd(0, E0)
-    run(stage4, edge1[2:])
     run(stage1, edge0)
 
     pl.semaphore_signal(csem.at[2], inc=1, device_id=partner, device_id_type=MESH)
@@ -584,7 +603,7 @@
         v((4, NN, NS, H), BF), v((4, NN, NS, H), F32),
         v((3, *node), BF), v((2, *node), BF), v((2, *node), F32), v((2, *node), F32),
         v(node, BF), v(node, F32), v((6, 16, D), F32),
-        dma((12,)), dma((14,)), dma((14,)), pltpu.SemaphoreType.REGULAR((3,)), dma((4,)),
+        dma((12,)), dma((19,)), dma((19,)), pltpu.SemaphoreType.REGULAR((3,)), dma((4,)),
         dma((7, 3)), dma((7, 9)), dma((7, 2)),
     ]
     return pl.pallas_call(

time: 173 us -> 170 us (0.983)
  Pallas kernels: 172 us -> 169 us
    pallas_call x1, Pallas kernels: 162 us -> 159 us  [compute(): pl.pallas_call(body, out_shape=[jax.ShapeDtypeStruct(*o) for o in outs],...]
where the time goes in v6:
time: 170 us; the launch traced here: 169 us
  Pallas kernels  169 us (99%)
    pallas_call x1, Pallas kernels, compute(): pl.pallas_call(body, out_shape=[jax.ShapeDtypeStruct(*o) for o in outs],...  159 us
    pallas_call x1, Pallas kernels, move(): pl.pallas_call(mover, out_shape=shapes, in_specs=[any_spec] * len(arrays)...  9.86 us

profile of v6, /device:TPU:0, one launch (start us, length us, event | category | flops | bytes accessed | tf_op | source)
XLA Modules:
  0.0 169.4 jit_solution(12778908882103944047)
XLA Ops:
  0.6 158.7 %shard_map.229 = (bf16[42,16,256]{2,1,0:T(8,128)(2,1)}, bf16[300,16,256]{2,1,0:T(8,128)(2,1)}, bf16[42,16,256]{2,1,0:T(8,128)(2,1)}, bf16[300,16,256]{2,1,0:T(8,...) custom-call(bf16[42,16,256]{2,1,0:T(8,128)(2,1)} %bitcast.14, ...), custom_call_target="tpu_custom_call" | custom-call | tf_op jit(solution)/shard_map/pallas_call | solution.py:609
  159.4 9.9 %shard_map.230 = (bf16[42,16,256]{2,1,0:T(8,128)(2,1)}, bf16[300,16,256]{2,1,0:T(8,128)(2,1)}, bf16[42,16,256]{2,1,0:T(8,128)(2,1)}, bf16[300,16,256]{2,1,0:T(8,...) custom-call(bf16[42,16,256]{2,1,0:T(8,128)(2,1)} %get-tuple-element., ...), custom_call_target="tpu_custom_call" | custom-call | tf_op jit(solution)/shard_map/pallas_call | solution.py:642

commit v7 on v6

--- a/solution.py
+++ b/solution.py
@@ -18,7 +18,7 @@
 PAIR = 2 * NS
 H = 256
 ROWS = NN * NS
-NB = 10
+NB = 5
 BE = NE // NB
 WIDE = 60
 
@@ -63,7 +63,7 @@
          o_n, o_e, o_dn, o_de, o_ew1, o_ew2, o_nw1, o_nw2, o_be, o_bn, o_ve, o_vn, spill,
          W1E, W2E, W1N, W2N, VE, VN, KS, KR,
          E0, E1, E2, DE, HS, CS, R2, G, PS, PR, GA, AG,
-         NST, NF, VF, SF, HN, CN, DN, DV, SM,
+         NST, NF, VF, SF, HN, CN, DN, SM,
          lsem, ssem, rsem, csem, spsem, gssem, grsem, osem):
     dp = lax.axis_index('dp')
     tp = lax.axis_index('tp')
@@ -400,8 +400,8 @@
     node1, edge1, node0, edge0 = (list(range(*ends)) for ends in ((0, 3), (3, 7), (7, 10), (10, 14)))
 
     plan = {
-        1: [(stage2, node1, 3), (stage3, node1, 7)],
-        0: [(stage2, edge1, 0), (stage5, node1, 3), (stage3, edge1, 5), (stage4, edge1[:2], 8)],
+        1: [(stage2, node1, 1), (stage3, node1[:2], 3)],
+        0: [(stage2, edge1, 0), (stage5, node1, 2), (stage3, edge1[:2], 3)],
     }
 
     def put_w2(layer, j, half, value, add):
@@ -453,7 +453,7 @@
         put_w1(layer, J_NW1 + 1, dot_rows(SF[layer], d_hid))
         stage0(nodes[2])
         stage1(nodes[1])
-        DV[...] = d_node + dot_cols(d_hid, full1(W1N, layer, 0))
+        HN[layer] = d_node + dot_cols(d_hid, full1(W1N, layer, 0))
         PS[...] = dot_cols(d_hid, full1(W1N, layer, 1)).reshape(NN, NS, D)
         stage1(nodes[2])
         for j in (J_EW2, J_EW1):
@@ -490,13 +490,14 @@
             for cp in fills:
                 cp.start()
         run(stage0, edge_w2 + edge_w1[:1])
-        run(stage4, node1[:2] if layer else edge1[2:])
+        run(stage3, (node1 if layer else edge1)[2:])
+        run(stage4, node1[:2] if layer else edge1)
         d_ps, d_pr = AG[...].astype(BF), rows_of(PR[...]).astype(BF)
         put_w1(layer, J_EW1 + 1, dot_rows(VF[layer], d_ps))
         stage0(edge_w1[1])
         put_w1(layer, J_EW1 + 2, dot_rows(VF[layer], d_pr))
         stage0(edge_w1[2])
-        DN[...] = (DV[...] + dot_cols(d_ps, full1(W1E, layer, 1))
+        DN[...] = (HN[layer] + dot_cols(d_ps, full1(W1E, layer, 1))
                    + dot_cols(d_pr, full1(W1E, layer, 2))).astype(BF)
 
     layer_bwd(1, E1)
@@ -602,7 +603,7 @@
         v((NN, NS, D), F32), v((NN, NS, D), F32), v((WIDE * NS, D), F32), v(node, F32),
         v((4, NN, NS, H), BF), v((4, NN, NS, H), F32),
         v((3, *node), BF), v((2, *node), BF), v((2, *node), F32), v((2, *node), F32),
-        v(node, BF), v(node, F32), v((6, 16, D), F32),
+        v(node, BF), v((6, 16, D), F32),
         dma((12,)), dma((19,)), dma((19,)), pltpu.SemaphoreType.REGULAR((3,)), dma((4,)),
         dma((7, 3)), dma((7, 9)), dma((7, 2)),
     ]

time: 170 us -> 169 us (level)
  no operation moved by 1% of the time
where the time goes in v7:
time: 169 us
  Pallas kernels  168 us (99%)
    pallas_call x1, Pallas kernels, compute(): pl.pallas_call(body, out_shape=[jax.ShapeDtypeStruct(*o) for o in outs],...  158 us
    pallas_call x1, Pallas kernels, move(): pl.pallas_call(mover, out_shape=shapes, in_specs=[any_spec] * len(arrays)...  9.86 us

profile of v7, /device:TPU:0, one launch (start us, length us, event | category | flops | bytes accessed | tf_op | source)
XLA Modules:
  0.0 168.8 jit_solution(8405874313884878859)
XLA Ops:
  0.6 158.1 %shard_map.229 = (bf16[42,16,256]{2,1,0:T(8,128)(2,1)}, bf16[300,16,256]{2,1,0:T(8,128)(2,1)}, bf16[42,16,256]{2,1,0:T(8,128)(2,1)}, bf16[300,16,256]{2,1,0:T(8,...) custom-call(bf16[42,16,256]{2,1,0:T(8,128)(2,1)} %bitcast.14, ...), custom_call_target="tpu_custom_call" | custom-call | tf_op jit(solution)/shard_map/pallas_call | solution.py:610
  158.8 9.9 %shard_map.230 = (bf16[42,16,256]{2,1,0:T(8,128)(2,1)}, bf16[300,16,256]{2,1,0:T(8,128)(2,1)}, bf16[42,16,256]{2,1,0:T(8,128)(2,1)}, bf16[300,16,256]{2,1,0:T(8,...) custom-call(bf16[42,16,256]{2,1,0:T(8,128)(2,1)} %get-tuple-element., ...), custom_call_target="tpu_custom_call" | custom-call | tf_op jit(solution)/shard_map/pallas_call | solution.py:643
